TPU v7x, 128 devices: a whole 4x4x4 slice. The times are simulated.
128 devices in a mesh: lat: 4 (over y), lon: 16 (over z, x), mem: 2 (over core).
Axes of the slice: x: 4, y: 4, z: 4, core: 2. Of those that a mesh axis runs over, the one named last changes fastest.
Arguments:
- anomalies: bfloat16 [24, 16, 1440, 512], P('mem', None, 'lon', 'lat'), may hold values from -6 to 6
- taper: float32 [16, 1440, 512], P('lon', 'lat'), may hold values from 0.5 to 8
- obs_row: int32 [256, 2048], P('lat', 'lon'), may hold values from 0 to 511, as said below
- obs_col: int32 [256, 2048], P('lat', 'lon'), may hold values from 0 to 1439, as said below
- obs_level: int32 [256, 2048], P('lat', 'lon'), may hold values from 0 to 15
- obs_value: float32 [256, 2048], P('lat', 'lon'), may hold values from -18 to 18
Outputs:
- increment: float32 [16, 1440, 512], P(None, 'lon', 'lat')
Inputs may be any that keep to these rules, and one draw needn't show every extreme that they name: `obs_row`: the entry in row i lies in latitude rows (i // 64) * 128 to (i // 64 + 1) * 128 - 1, drawn evenly there. `obs_col`: the entry in column j lies in longitude columns (j // 128) * 90 to (j // 128 + 1) * 90 - 1, drawn evenly there.
All inputs are finite; a program needn't handle non-finite values.
Results may differ from a plain program's by a relative error of at most 0.0066.
Values may be sent and summed in bfloat16 or wider, within the bound.
No kernel may reach another device: no remote copies, remote signals or barrier semaphores. Data moves between devices by JAX's collectives and lax.ppermute only.
A program may use at most 128 MiB of HBM per device.

v0:
```python
import math

import jax
import jax.numpy as jnp
from jax import lax
from jax.experimental import pallas as pl
from jax.experimental.pallas import tpu as pltpu
from jax.sharding import PartitionSpec as P


BF = jnp.bfloat16
F32 = jnp.float32
LL = ("lat", "lon")
SWAP = [(0, 1), (1, 0)]
RING = 4


def vspec():
    return pl.BlockSpec(memory_space=pltpu.VMEM)


def sspec():
    return pl.BlockSpec(memory_space=pltpu.SMEM)


def params(mib, **more):
    return pltpu.CompilerParams(vmem_limit_bytes=mib * 1024 * 1024, **more)


def cost(flops):
    return pl.CostEstimate(flops=int(flops), bytes_accessed=1 << 20, transcendentals=0)


def over_all(x):
    return lax.all_to_all(x, LL, split_axis=0, concat_axis=0, tiled=True)


def shift_lat(x, s):
    return lax.ppermute(x, "lat", [(i, (i + s) % RING) for i in range(RING)])


def swap(x):
    return lax.ppermute(x, "mem", SWAP)


def turn_block(blocks, turn, levels):
    have = blocks[0].shape[0]
    both = jnp.concatenate([block.reshape(have * levels, 128) for block in blocks], axis=1)
    if have < 16:
        both = jnp.concatenate([both, jnp.zeros(((16 - have) * levels, 256), BF)], axis=0)
    return jnp.dot(turn, both, preferred_element_type=F32).astype(BF)


def turner(levels):
    size = 16 * levels
    to = lax.broadcasted_iota(jnp.int32, (size, size), 0)
    frm = lax.broadcasted_iota(jnp.int32, (size, size), 1)
    return jnp.where(frm == (to & 15) * levels + (to >> 4), 1.0, 0.0).astype(BF)


def head_kernel(place, fields, row_hbm, col_hbm, level_hbm, value_hbm, out, *scratch, half, levels, cols, padded):
    row_ref, col_ref, level_ref, value_ref, fields_in, staged, innov, acc, sems = scratch
    bands = fields.shape[1]
    count = iter(range(32))

    def fetch(source, target):
        copy = pltpu.make_async_copy(source, target, sems.at[next(count)])
        copy.start()
        return copy

    observed = [
        fetch(row_hbm, row_ref),
        fetch(col_hbm, col_ref),
        fetch(level_hbm, level_ref),
        fetch(value_hbm, value_ref),
    ]
    arriving = [fetch(fields.at[pl.ds(0, 2), g], fields_in.at[:, g]) for g in range(bands)]
    mem, lat, lon = place[0], place[1], place[2]
    slots = levels * half
    col_start = lon * cols + mem * half
    acc[...] = jnp.zeros_like(acc)
    slot_ids = lax.broadcasted_iota(jnp.int32, (slots, 128), 0)
    row_ids = lax.broadcasted_iota(jnp.int32, (128, 128), 0)
    for copy in observed:
        copy.wait()

    def add_group(g, carry):
        rows = pl.ds(pl.multiple_of(g * 8, 8), 8)
        within = col_ref[rows, :] - col_start
        inside = (within >= 0) & (within < half)
        keys = jnp.where(inside, level_ref[rows, :] * half + within, -1)
        lat_row = row_ref[rows, :] - lat * 128
        value = value_ref[rows, :]
        high = value.astype(BF).astype(F32)
        middle = value - high
        left = []
        right = []
        for r in range(8):
            hit = slot_ids == keys[r : r + 1, :]
            left.append(jnp.where(hit, 1.0, 0.0).astype(BF))
            row_hit = row_ids == lat_row[r : r + 1, :]
            top = jnp.where(row_hit, high[r : r + 1, :], 0.0)
            low = jnp.where(row_hit, middle[r : r + 1, :], 0.0)
            right.append(jnp.concatenate([top, low], axis=0).astype(BF))
        acc[...] += lax.dot_general(
            jnp.concatenate(left, axis=1),
            jnp.concatenate(right, axis=1),
            (((1,), (1,)), ((), ())),
            preferred_element_type=F32,
        )
        return carry

    lax.fori_loop(0, row_ref.shape[0] // 8, add_group, 0)
    innov[...] = (acc[:, :128] + acc[:, 128:]).astype(BF).reshape(levels, half, 128)
    leaving = [
        fetch(innov, out.at[pl.ds(g * levels, levels), pl.ds(2 * padded, half), :]) for g in range(bands)
    ]
    turn = turner(levels)
    for g in range(bands):
        arriving[g].wait()
        for start in range(0, padded, 16):
            have = min(16, cols - start)
            turned = turn_block([fields_in[p, g, start : start + have] for p in range(2)], turn, levels)
            for l in range(levels):
                for p in range(2):
                    piece = turned[16 * l : 16 * l + 16, 128 * p : 128 * p + 128]
                    staged[g * levels + l, p * padded + start : p * padded + start + 16, :] = piece
        leaving.append(
            fetch(
                staged.at[pl.ds(g * levels, levels)],
                out.at[pl.ds(g * levels, levels), pl.ds(0, 2 * padded), :],
            )
        )
    for copy in leaving:
        copy.wait()


def head(place, fields, obs_row, obs_col, obs_level, obs_value, half, padded):
    _, bands, cols, levels, lanes = fields.shape
    rows = 2 * padded + half
    hbm = pl.BlockSpec(memory_space=pltpu.HBM)
    observed = (obs_row, obs_col, obs_level, obs_value)
    return pl.pallas_call(
        lambda *refs: head_kernel(*refs, half=half, levels=levels, cols=cols, padded=padded),
        out_shape=jax.ShapeDtypeStruct((bands * levels, rows, lanes), BF),
        in_specs=[sspec()] + [hbm] * 5,
        out_specs=hbm,
        scratch_shapes=[pltpu.VMEM(array.shape, array.dtype) for array in observed]
        + [
            pltpu.VMEM((2, bands, cols, levels, lanes), BF),
            pltpu.VMEM((bands * levels, 2 * padded, lanes), BF),
            pltpu.VMEM((levels, half, lanes), BF),
            pltpu.VMEM((levels * half, 2 * lanes), F32),
            pltpu.SemaphoreType.DMA((32,)),
        ],
        compiler_params=params(61),
        cost_estimate=cost(6e9),
        name="head",
    )(place, fields, *observed)


def relayout_last_kernel(in_ref, out_ref, *, cols, levels, padded):
    turn = turner(levels)
    for start in range(0, padded, 16):
        have = min(16, cols - start)
        turned = turn_block([in_ref[0, p, start : start + have] for p in range(2)], turn, levels)
        for l in range(levels):
            for p in range(2):
                piece = turned[16 * l : 16 * l + 16, 128 * p : 128 * p + 128]
                out_ref[p * levels + l, start : start + 16, :] = piece


def relayout_last(fields, padded):
    rounds, bands, cols, levels, lanes = fields.shape
    return pl.pallas_call(
        lambda i, o: relayout_last_kernel(i, o, cols=cols, levels=levels, padded=padded),
        grid=(bands // 2,),
        in_specs=[pl.BlockSpec((1, 2, cols, levels, lanes), lambda g: (rounds - 1, g, 0, 0, 0))],
        out_specs=pl.BlockSpec((2 * levels, padded, lanes), lambda g: (g, 0, 0)),
        out_shape=jax.ShapeDtypeStruct((bands * levels, padded, lanes), BF),
        compiler_params=params(58),
        name="relayout_last",
    )(fields)


def turn_cos(turns):
    near = 0.25 - jnp.abs(turns - jnp.floor(turns + 0.5))
    square = near * near
    value = jnp.full_like(square, -15.094642576822990)
    for factor in (42.058693944897653, -76.705859753061386, 81.605249276075055, -41.341702240399755):
        value = value * square + factor
    return near * (value * square + 6.283185307179586)


def basis_kernel(lon_ref, lon_t_ref, lat_ref, lat_t_ref, *, cols, blocks, padded):
    total = cols * blocks
    half = total // 2
    tiles = lon_ref.shape[1] // 128
    lanes = lax.broadcasted_iota(jnp.int32, (padded, 128), 1)

    def turns_of(product):
        whole = (product.astype(F32) * (1.0 / total)).astype(jnp.int32)
        return (product - whole * total).astype(F32) * (1.0 / total)

    def lon_rows(j, carry):
        within = lax.broadcasted_iota(jnp.int32, (padded, 128), 0)
        x = within + cols * j
        fine = turns_of(x * lanes)
        coarse = turns_of(x * (lanes * 128))
        fine_cos = turn_cos(fine)
        fine_sin = turn_cos(fine - 0.25)
        scale = jnp.where(within < cols, math.sqrt(2.0 / total), 0.0)
        coarse_cos = turn_cos(coarse) * scale
        coarse_sin = turn_cos(coarse - 0.25) * scale
        sign = jnp.where((x & 1) == 0, 1.0, -1.0)
        rows = pl.ds(pl.multiple_of(j * padded, padded), padded)
        for t in range(tiles):
            c = lanes + 128 * t
            cos_t = coarse_cos[:, t : t + 1]
            sin_t = coarse_sin[:, t : t + 1]
            parts = []
            if 128 * t <= half:
                parts.append(fine_cos * cos_t - fine_sin * sin_t)
            if 128 * t + 127 > half:
                parts.append((fine_sin * cos_t + fine_cos * sin_t) * sign)
            value = parts[0] if len(parts) == 1 else jnp.where(c <= half, parts[0], parts[1])
            if t == 0 or 128 * t <= half < 128 * t + 128:
                value = jnp.where((c == 0) | (c == half), value * math.sqrt(0.5), value)
            if 128 * t + 127 >= total:
                value = jnp.where(c < total, value, 0.0)
            lon_ref[rows, 128 * t : 128 * t + 128] = value.astype(BF)
        return carry

    lax.fori_loop(0, blocks, lon_rows, 0)
    for t in range(tiles):
        strip = lon_ref[:, 128 * t : 128 * t + 128].astype(F32)
        lon_t_ref[128 * t : 128 * t + 128, :] = strip.T.astype(BF)

    length = lat_ref.shape[0]
    step = 64

    def lat_rows(i, carry):
        shape = (step, length)
        down = lax.broadcasted_iota(jnp.int32, shape, 0) + step * i
        across = lax.broadcasted_iota(jnp.int32, shape, 1)
        rows = pl.ds(pl.multiple_of(i * step, step), step)
        for grid, mode, ref in ((down, across, lat_ref), (across, down, lat_t_ref)):
            phase = (mode * (2 * grid + 1)) & (4 * length - 1)
            scale = jnp.where(mode == 0, 1.0 / math.sqrt(length), math.sqrt(2.0 / length))
            ref[rows, :] = (turn_cos(phase.astype(F32) * (0.25 / length)) * scale).astype(BF)
        return carry

    lax.fori_loop(0, length // step, lat_rows, 0)


def bases(cols, blocks, padded, lat_total):
    wide = padded * blocks
    return pl.pallas_call(
        lambda *refs: basis_kernel(*refs, cols=cols, blocks=blocks, padded=padded),
        out_shape=(
            jax.ShapeDtypeStruct((wide, wide), BF),
            jax.ShapeDtypeStruct((wide, wide), BF),
            jax.ShapeDtypeStruct((lat_total, lat_total), BF),
            jax.ShapeDtypeStruct((lat_total, lat_total), BF),
        ),
        out_specs=(vspec(),) * 4,
        compiler_params=params(58),
        cost_estimate=cost(12e9),
        name="bases",
    )()


def arrange_kernel(place, own, other, taper, *, rows_each):
    mem, lat = place[0], place[1]
    for ref, side in ((own, mem), (other, 1 - mem)):
        for u in range(RING):
            into = pl.ds(pl.multiple_of(lax.rem(lat + RING - u, RING) * rows_each, 8), rows_each)
            for q in range(2):
                taper[2 * side + q, into, :] = ref[u, :, 128 * q : 128 * q + 128]


def arrange(place, own, other):
    rows_each = own.shape[1]
    return pl.pallas_call(
        lambda *refs: arrange_kernel(*refs, rows_each=rows_each),
        out_shape=jax.ShapeDtypeStruct((4, RING * rows_each, 128), BF),
        in_specs=[sspec(), vspec(), vspec()],
        out_specs=vspec(),
        compiler_params=params(12),
        cost_estimate=cost(1e9),
        name="arrange",
    )(place, own, other)


def member_kernel(*refs, first, final, count, blocks, bands, padded, coefs):
    place, field_hbm, pair_hbm, other_hbm, taper_hbm, lon_hbm, lon_t_hbm, lat_hbm, lat_t_hbm = refs[:9]
    rest = list(refs[9:])
    so_far_hbm = None if first else rest.pop(0)
    outs = [rest.pop(0) for _ in range(2 if final else 1)]
    weighted, inverse, field, innov, taper, lon_ref, lon_t_ref, lat_ref, lat_t_ref, acc, sems = rest[:11]
    stages = rest[11:] if final else [acc]
    wide = padded * blocks
    parts = 3
    step = coefs // parts
    group = 4
    turns = blocks // group
    tall = group * padded
    half = padded // 2
    mem = place[0]
    own_rows = pl.ds(pl.multiple_of(mem * half, half), half)
    other_rows = pl.ds(pl.multiple_of((1 - mem) * half, half), half)

    def move(source, target, spot):
        return pltpu.make_async_copy(source, target, sems.at[spot])

    def lon_t_copy(r):
        rows = pl.ds(pl.multiple_of(r * step, 16), step)
        return move(lon_t_hbm.at[rows], lon_t_ref.at[rows], 10 + r)

    def lon_copy(b):
        rows = pl.ds(pl.multiple_of(b * tall, tall), tall)
        return move(lon_hbm.at[rows], lon_ref.at[rows], 14 + b)

    def so_far_copy(b):
        return move(so_far_hbm.at[:, pl.ds(b * group, group)], acc.at[:, pl.ds(b * group, group)], 18 + b)

    def out_copy(b, n):
        spots = pl.ds(b * group, group)
        return move(stages[n].at[:, spots], outs[n].at[:, spots], 22 + 4 * n + b)

    innov_copies = [
        move(pair_hbm.at[:, :, pl.ds(2 * padded, half), :], innov.at[:, :, own_rows, :], 0),
        move(other_hbm, innov.at[:, :, other_rows, :], 1),
    ]
    field_copies = [
        move(field_hbm.at[a, :, pl.ds(0, count * padded), :], field.at[a], 2 + a) for a in range(bands)
    ]
    table_copies = [
        lon_t_copy(0),
        move(lat_hbm, lat_ref, 7),
        move(taper_hbm, taper, 8),
        move(lat_t_hbm, lat_t_ref, 9),
    ]
    for copy in innov_copies + field_copies + table_copies:
        copy.start()
    inverse[coefs:, :] = jnp.zeros((wide - coefs, inverse.shape[1]), BF)
    for copy in innov_copies:
        copy.wait()

    def weigh(i, a):
        def body(j, carry):
            rows = pl.ds(pl.multiple_of(j * padded, padded), padded)
            product = field[a, j, i * padded : (i + 1) * padded, :] * innov[a, j]
            weighted[rows, 128 * a : 128 * a + 128] = product
            return carry

        lax.fori_loop(0, blocks, body, 0)

    def spectral(fresh):
        def body(r, carry):
            rows = pl.ds(pl.multiple_of(r * step, 16), step)
            if fresh:

                @pl.when(r > 0)
                def _():
                    lon_t_copy(r).wait()

            zonal = jnp.dot(lon_t_ref[rows, :], weighted[...], preferred_element_type=F32).astype(BF)
            spectrum = jnp.dot(zonal, lat_ref[...], preferred_element_type=F32)
            weights = jnp.concatenate([taper[q, rows, :] for q in range(4)], axis=1).astype(F32)
            tapered = (spectrum * weights).astype(BF)
            inverse[rows, :] = jnp.dot(tapered, lat_t_ref[...], preferred_element_type=F32).astype(BF)
            if fresh:

                @pl.when(r == 0)
                def _():
                    for b in range(turns):
                        lon_copy(b).start()
                        if not first:
                            so_far_copy(b).start()

            return carry

        lax.fori_loop(0, parts, body, 0)

    def gridded(i):
        def body(b, carry):
            rows = pl.ds(pl.multiple_of(b * tall, tall), tall)
            if i == 0:
                lon_copy(b).wait()
                if not first:
                    so_far_copy(b).wait()
            localized = jnp.dot(lon_ref[rows, :], inverse[...], preferred_element_type=F32)
            for g in range(group):
                for a in range(bands):
                    j = b * group + g
                    piece = localized[g * padded : (g + 1) * padded, 128 * a : 128 * a + 128]
                    piece = piece * field[a, j, i * padded : (i + 1) * padded, :].astype(F32)
                    piece = piece if first and i == 0 else piece + acc[a, j]
                    if final:
                        top, low = piece[:half], piece[half:]
                        stages[0][a, j] = jnp.where(mem == 0, top, low).astype(BF)
                        stages[1][a, j] = jnp.where(mem == 0, low, top).astype(BF)
                    else:
                        acc[a, j] = piece
            if i == count - 1:
                for n in range(len(outs)):
                    out_copy(b, n).start()
            return carry

        lax.fori_loop(0, turns, body, 0)

    for i in range(count):
        for a in range(bands):
            if i == 0:
                field_copies[a].wait()
            weigh(i, a)
        if i == 0:
            for r in range(1, parts):
                lon_t_copy(r).start()
            for copy in table_copies:
                copy.wait()
        spectral(i == 0)
        gridded(i)
    for b in range(turns):
        for n in range(len(outs)):
            out_copy(b, n).wait()


def member(place, field, pair, other, taper, tables, so_far, final, dims):
    _, blocks, bands, padded, coefs, lat_total = dims
    half = padded // 2
    wide = padded * blocks
    first = so_far is None
    count = 1 if final else 2
    split = lambda array: array.reshape(bands, blocks, *array.shape[1:])
    far = [split(field), split(pair), split(other), taper, *tables] + ([] if first else [so_far])
    block = lambda rows, dtype: ((bands, blocks, rows, 128), dtype)
    scratch = [((wide, lat_total), BF), ((wide, lat_total), BF), block(count * padded, BF), block(padded, BF)]
    scratch += [(array.shape, array.dtype) for array in (taper, *tables)]
    scratch.append(block(padded, F32))
    results = [block(half, BF), block(half, BF)] if final else [block(padded, F32)]
    hbm = pl.BlockSpec(memory_space=pltpu.HBM)
    return pl.pallas_call(
        lambda *refs: member_kernel(
            *refs, first=first, final=final, count=count, blocks=blocks, bands=bands, padded=padded, coefs=coefs
        ),
        out_shape=[jax.ShapeDtypeStruct(*each) for each in results],
        in_specs=[sspec()] + [hbm] * len(far),
        out_specs=[hbm] * len(results),
        scratch_shapes=[pltpu.VMEM(*each) for each in scratch]
        + [pltpu.SemaphoreType.DMA((32,))]
        + ([pltpu.VMEM(*each) for each in results] if final else []),
        compiler_params=params(60),
        cost_estimate=cost(count * 6e9),
        name="member_last" if final else "member_pair",
    )(place, *far)


def finish_kernel(place, own, other, out, *, levels, cols, half, scale):
    mem = place[0]
    bands = own.shape[0] // levels
    for side in range(2):
        rows = min(half, cols - side * half)
        for l in range(levels):
            mine = sum(own[a * levels + l].astype(F32) for a in range(bands))
            theirs = sum(other[a * levels + l].astype(F32) for a in range(bands))
            total = jnp.where(mem == side, mine, theirs) * scale
            out[side * half : side * half + rows, l, :] = total[:rows]


def finish(place, own, other, levels, cols, half, scale):
    return pl.pallas_call(
        lambda *refs: finish_kernel(*refs, levels=levels, cols=cols, half=half, scale=scale),
        out_shape=jax.ShapeDtypeStruct((cols, levels, 128), F32),
        in_specs=[sspec(), vspec(), vspec()],
        out_specs=vspec(),
        compiler_params=params(12),
        name="finish",
    )(place, own, other)


def local(anomalies, taper, obs_row, obs_col, obs_level, obs_value):
    members, levels, cols, lat_rows = anomalies.shape
    bands = lax.axis_size("lat")
    blocks = lax.axis_size("lon")
    mem, lat, lon = lax.axis_index("mem"), lax.axis_index("lat"), lax.axis_index("lon")
    coefs = cols * blocks
    lat_total = lat_rows * bands
    padded = -(-cols // 32) * 32
    half = padded // 2
    ensemble = members * lax.axis_size("mem")
    place = jnp.stack([mem, lat, lon]).astype(jnp.int32)

    by_round = jnp.transpose(anomalies, (0, 2, 1, 3)).reshape(members // bands, bands, cols, levels, lat_rows)
    pair_out = head(place, by_round, obs_row, obs_col, obs_level, obs_value, half, padded)
    pair = over_all(pair_out)
    n_half = lat_total // 2
    taper_mine = lax.dynamic_slice_in_dim(taper[0], mem * n_half, n_half, axis=1).astype(BF)
    ring = [taper_mine]
    for u in range(1, RING):
        ring.append(shift_lat(taper_mine, u))
    last_out = relayout_last(by_round, padded)
    last = over_all(last_out)
    own = jnp.stack(ring)
    weights = arrange(place, own, swap(own))
    other = swap(pair[:, 2 * padded :, :])

    tables = bases(cols, blocks, padded, lat_total)
    dims = (cols, blocks, bands, padded, coefs, lat_total)
    (summed,) = member(place, pair, pair, other, weights, tables, None, False, dims)
    mine, theirs = member(place, last, pair, other, weights, tables, summed, True, dims)
    merged = (mine.astype(F32) + swap(theirs).astype(F32)).astype(BF).reshape(bands * blocks, half, lat_rows)
    pieces = over_all(merged)
    out = finish(place, pieces, swap(pieces), levels, cols, half, 1.0 / (ensemble - 1))
    return jnp.transpose(out, (1, 0, 2))


def solution(mesh):
    in_specs = (
        P("mem", None, "lon", "lat"),
        P("lon", "lat", None),
        P("lat", "lon"),
        P("lat", "lon"),
        P("lat", "lon"),
        P("lat", "lon"),
    )
    out_specs = P(None, "lon", "lat")

    return jax.shard_map(local, mesh=mesh, in_specs=in_specs, out_specs=out_specs, check_vma=False)
```

profile of v0, /device:TPU:1, one launch (start us, length us, event | category | flops | bytes accessed | tf_op | source)
XLA Modules:
  0.0 173.8 jit_solution(17241481922331082120)
XLA Ops:
  0.0 0.0 copy-start
  0.0 0.6 pad_add_fusion.refs_0_
  0.6 9.3 %head.1 = bf16[64,240,128]{2,1,0:T(8,128)(2,1)} custom-call(s32[3]{0:T(128)} %pad_add_fusion.refs_0_, bf16[3,4,90,16,128]{4,3,2,1,0:T(8,128)(2,1)} %bitcast.16, s32[64,128]{1,0:T(8,128)} %refs_2_.1, s32[64,128]{1,0:T(8,128)} %refs_3_.1, s32[64,128]{1,0:T(8,128)} %refs_4_.1, f32[64,128]{1,0:T(8,128)} %refs_5_.1), custom_call_target="tpu_custom_call" | custom-call | flops 6000000000 | bytes 1048576 | tf_op jit(solution)/shard_map/head/pallas_call | solution.py:143
  9.9 12.2 %all-to-all-start.1 = ((bf16[64,240,128]{2,1,0:T(8,128)(2,1)}), bf16[64,240,128]{2,1,0:T(8,128)(2,1)}, u32[]{:S(2)}, u32[]{:S(2)}) async-start(bf16[64,240,128]{2,1,0:T(8,128)(2,1)} %head.1), calls=%async_computation.1 | async-start | bytes 7864320 | tf_op jit(solution)/shard_map/all_to_all | solution.py:35
  22.1 0.0 copy-done
  22.1 2.4 %collective-permute-start.3 = (bf16[360,256]{1,0:T(8,128)(2,1)S(1)}, bf16[360,256]{1,0:T(8,128)(2,1)S(1)}, u32[]{:S(2)}, u32[]{:S(2)}) collective-permute-start(bf16[360,256]{1,0:T(8,128)(2,1)S(1)} %fusion), channel_id=1, source_target_pairs={{0,96},{32,0},{64,32},{96,64},{1,97},{33,1},{65,33},{97,65},{2,98}... | collective-permute-start | bytes 552968 | tf_op jit(solution)/shard_map/ppermute | solution.py:39
  24.5 0.4 collective-permute-start.2
  24.9 0.7 collective-permute-start.1
  25.6 2.8 %relayout_last.1 = bf16[64,96,128]{2,1,0:T(8,128)(2,1)} custom-call(bf16[3,4,90,16,128]{4,3,2,1,0:T(8,128)(2,1)} %bitcast.17), custom_call_target="tpu_custom_call" | custom-call | tf_op jit(solution)/shard_map/relayout_last/pallas_call | solution.py:175
  28.4 41.0 %collective-permute-done.3 = bf16[360,256]{1,0:T(8,128)(2,1)S(1)} collective-permute-done((bf16[360,256]{1,0:T(8,128)(2,1)S(1)}, bf16[360,256]{1,0:T(8,128)(2,1)S(1)}, u32[]{:S(2)}, u32[]{:S(2)}) %collective-permute-start.3) | collective-permute-done | bytes 184352 | tf_op jit(solution)/shard_map/ppermute | solution.py:39
  69.4 2.2 %collective-permute-done.2 = bf16[360,256]{1,0:T(8,128)(2,1)S(1)} collective-permute-done((bf16[360,256]{1,0:T(8,128)(2,1)S(1)}, bf16[360,256]{1,0:T(8,128)(2,1)S(1)}, u32[]{:S(2)}, u32[]{:S(2)}) %collective-permute-start.2) | collective-permute-done | bytes 184352 | tf_op jit(solution)/shard_map/ppermute | solution.py:39
  71.6 3.3 %collective-permute-done.1 = bf16[360,256]{1,0:T(8,128)(2,1)S(1)} collective-permute-done((bf16[360,256]{1,0:T(8,128)(2,1)S(1)}, bf16[360,256]{1,0:T(8,128)(2,1)S(1)}, u32[]{:S(2)}, u32[]{:S(2)}) %collective-permute-start.1) | collective-permute-done | bytes 184352 | tf_op jit(solution)/shard_map/ppermute | solution.py:39
  74.9 0.1 pad_maximum_fusion.refs_1_
  75.0 1.4 collective-permute-start.4
  76.4 0.0 all-to-all-done.1
  76.4 10.8 %all-to-all-start = ((bf16[64,96,128]{2,1,0:T(8,128)(2,1)}), bf16[64,96,128]{2,1,0:T(8,128)(2,1)}, u32[]{:S(2)}, u32[]{:S(2)}) async-start(bf16[64,96,128]{2,1,0:T(8,128)(2,1)} %relayout_last.1), calls=%async_computation | async-start | bytes 3145728 | tf_op jit(solution)/shard_map/all_to_all | solution.py:35
  87.2 1.2 slice.4
  88.4 0.0 copy-start.1
  88.4 0.6 collective-permute-start
  89.0 14.0 %bases.1 = (bf16[1536,1536]{1,0:T(8,128)(2,1)}, bf16[1536,1536]{1,0:T(8,128)(2,1)}, bf16[512,512]{1,0:T(8,128)(2,1)}, bf16[512,512]{1,0:T(8,128)(2,1)}) custom-call(), custom_call_target="tpu_custom_call" | custom-call | flops 12000000000 | bytes 1048576 | tf_op jit(solution)/shard_map/bases/pallas_call | solution.py:258
  102.9 0.0 collective-permute-done.4.refs_2_
  102.9 0.0 copy-done.1
  102.9 0.8 arrange.1.refs_4_
  103.8 0.0 copy-start.3
  103.8 1.1 copy-done.3
  104.9 0.0 collective-permute-done
  104.9 0.0 copy-start.4
  104.9 0.9 copy-done.4
  105.8 20.9 %member_pair.1.refs_9_ = f32[4,16,96,128]{3,2,1,0:T(8,128)} custom-call(s32[3]{0:T(128)} %pad_add_fusion.refs_0_, bf16[4,16,240,128]{3,2,1,0:T(8,128)(2,1)} %bitcast.7.refs_1_.refs_2_, bf16[4,16,240,128]{3,2,1,0:T(8,128)(2,1)} %bitcast.7.refs_1_.refs_2_, bf16[4,16,48,128]{3,2,1,0:T(8,128)(2,1)} %bitcast.22, bf16[4,1440,128]{2,1,0:T(8,128)(2,1)} %copy-done.3, ...), custom_call_target="tpu_custom_call" | custom-call | flops 12000000000 | bytes 1048576 | tf_op jit(solution)/shard_map/member_pair/pallas_call | solution.py:444
  126.7 0.0 all-to-all-done
  126.7 12.2 %member_last.1 = (bf16[4,16,48,128]{3,2,1,0:T(8,128)(2,1)}, bf16[4,16,48,128]{3,2,1,0:T(8,128)(2,1)}) custom-call(s32[3]{0:T(128)} %pad_add_fusion.refs_0_, bf16[4,16,96,128]{3,2,1,0:T(8,128)(2,1)} %bitcast.5.refs_1_, bf16[4,16,240,128]{3,2,1,0:T(8,128)(2,1)} %bitcast.7.refs_1_.refs_2_, bf16[4,16,48,128]{3,2,1,0:T(8,128)(2,1)} %bitcast.23, ...), custom_call_target="tpu_custom_call" | custom-call | flops 6000000000 | bytes 1048576 | tf_op jit(solution)/shard_map/member_last/pallas_call | solution.py:444
  138.9 0.0 copy-start.2
  138.9 0.3 collective-permute-start.5
  139.2 2.3 %collective-permute-done.5 = bf16[4,16,48,128]{3,2,1,0:T(8,128)(2,1)S(1)} collective-permute-done((bf16[4,16,48,128]{3,2,1,0:T(8,128)(2,1)}, bf16[4,16,48,128]{3,2,1,0:T(8,128)(2,1)S(1)}, u32[]{:S(2)}, u32[]{:S(2)}) %collective-permute-start.5) | collective-permute-done | bytes 786464 | tf_op jit(solution)/shard_map/ppermute | solution.py:43
  141.5 1.3 add_convert_fusion
  142.8 25.3 %all_to_all.15.refs_1_ = bf16[64,48,128]{2,1,0:T(8,128)(2,1)S(1)} all-to-all(bf16[64,48,128]{2,1,0:T(8,128)(2,1)S(1)} %bitcast.18), channel_id=1, replica_groups=mesh['lat'=4,'lon'=16,'mem'=2] {'lat','lon'}, dimensions={0} | all-to-all | bytes 1572864 | tf_op jit(solution)/shard_map/all_to_all | solution.py:35
  168.2 1.6 collective-permute-start.6
  169.8 1.9 %collective-permute-done.6.refs_2_ = bf16[64,48,128]{2,1,0:T(8,128)(2,1)S(1)} collective-permute-done((bf16[64,48,128]{2,1,0:T(8,128)(2,1)S(1)}, bf16[64,48,128]{2,1,0:T(8,128)(2,1)S(1)}, u32[]{:S(2)}, u32[]{:S(2)}) %collective-permute-start.6) | collective-permute-done | bytes 786464 | tf_op jit(solution)/shard_map/ppermute | solution.py:43
  171.7 0.0 copy-done.2
  171.7 2.1 %finish.1 = f32[90,16,128]{2,1,0:T(8,128)} custom-call(s32[3]{0:T(128)S(1)} %copy-done.2, bf16[64,48,128]{2,1,0:T(8,128)(2,1)S(1)} %all_to_all.15.refs_1_, bf16[64,48,128]{2,1,0:T(8,128)(2,1)S(1)} %collective-permute-done.6.refs_2_), custom_call_target="tpu_custom_call" | custom-call | tf_op jit(solution)/shard_map/finish/pallas_call | solution.py:473
  (2 shorter events, 0.1 us)
Async XLA Ops:
  0.0 22.1 %copy-start = (f32[1,360,512]{2,1,0:T(8,128)S(1)}, f32[1,360,512]{2,1,0:T(8,128)}, u32[]{:S(2)}) copy-start(f32[1,360,512]{2,1,0:T(8,128)} %param.7) | copy-start | bytes 2211844
  9.9 66.5 %all-to-all-start.1 = ((bf16[64,240,128]{2,1,0:T(8,128)(2,1)}), bf16[64,240,128]{2,1,0:T(8,128)(2,1)}, u32[]{:S(2)}, u32[]{:S(2)}) async-start(bf16[64,240,128]{2,1,0:T(8,128)(2,1)} %head.1), calls=%async_computation.1 | async-start | bytes 7864320 | tf_op jit(solution)/shard_map/all_to_all | solution.py:35
  22.1 47.2 %collective-permute-start.3 = (bf16[360,256]{1,0:T(8,128)(2,1)S(1)}, bf16[360,256]{1,0:T(8,128)(2,1)S(1)}, u32[]{:S(2)}, u32[]{:S(2)}) collective-permute-start(bf16[360,256]{1,0:T(8,128)(2,1)S(1)} %fusion), channel_id=1, source_target_pairs={{0,96},{32,0},{64,32},{96,64},{1,97},{33,1},{65,33},{97,65},{2,98}... | collective-permute-start | bytes 552968 | tf_op jit(solution)/shard_map/ppermute | solution.py:39
  24.5 47.0 %collective-permute-start.2 = (bf16[360,256]{1,0:T(8,128)(2,1)S(1)}, bf16[360,256]{1,0:T(8,128)(2,1)S(1)}, u32[]{:S(2)}, u32[]{:S(2)}) collective-permute-start(bf16[360,256]{1,0:T(8,128)(2,1)S(1)} %fusion), channel_id=1, source_target_pairs={{0,64},{32,96},{64,0},{96,32},{1,65},{33,97},{65,1},{97,33},{2,66}... | collective-permute-start | bytes 552968 | tf_op jit(solution)/shard_map/ppermute | solution.py:39
  24.9 49.9 %collective-permute-start.1 = (bf16[360,256]{1,0:T(8,128)(2,1)S(1)}, bf16[360,256]{1,0:T(8,128)(2,1)S(1)}, u32[]{:S(2)}, u32[]{:S(2)}) collective-permute-start(bf16[360,256]{1,0:T(8,128)(2,1)S(1)} %fusion), channel_id=1, source_target_pairs={{0,32},{32,64},{64,96},{96,0},{1,33},{33,65},{65,97},{97,1},{2,34}... | collective-permute-start | bytes 552968 | tf_op jit(solution)/shard_map/ppermute | solution.py:39
  75.0 28.0 %collective-permute-start.4 = (bf16[4,360,256]{2,1,0:T(8,128)(2,1)S(1)}, bf16[4,360,256]{2,1,0:T(8,128)(2,1)S(1)}, u32[]{:S(2)}, u32[]{:S(2)}) collective-permute-start(bf16[4,360,256]{2,1,0:T(8,128)(2,1)S(1)} %pad_maximum_fusion.refs_1_), channel_id=1, source_target_pairs={{0,1},{1,0},{2,3},{3,2},{4,5},{5,4},{6,7},{7,6},{8,9},{9,8},{10,11... | collective-permute-start | bytes 2211848 | tf_op jit(solution)/shard_map/ppermute | solution.py:43
  76.4 50.3 %all-to-all-start = ((bf16[64,96,128]{2,1,0:T(8,128)(2,1)}), bf16[64,96,128]{2,1,0:T(8,128)(2,1)}, u32[]{:S(2)}, u32[]{:S(2)}) async-start(bf16[64,96,128]{2,1,0:T(8,128)(2,1)} %relayout_last.1), calls=%async_computation | async-start | bytes 3145728 | tf_op jit(solution)/shard_map/all_to_all | solution.py:35
  88.4 14.5 %copy-start.1 = (s32[3]{0:T(128)S(1)}, s32[3]{0:T(128)}, u32[]{:S(2)}) copy-start(s32[3]{0:T(128)} %pad_add_fusion.refs_0_) | copy-start | bytes 40
  88.4 16.5 %collective-permute-start = (bf16[64,48,128]{2,1,0:T(8,128)(2,1)S(1)}, bf16[64,48,128]{2,1,0:T(8,128)(2,1)S(1)}, u32[]{:S(2)}, u32[]{:S(2)}) collective-permute-start(bf16[64,48,128]{2,1,0:T(8,128)(2,1)S(1)} %slice.4), channel_id=1, source_target_pairs={{0,1},{1,0},{2,3},{3,2},{4,5},{5,4},{6,7},{7,6},{8,9},{9,8},{10,11... | collective-permute-start | bytes 2359304 | tf_op jit(solution)/shard_map/ppermute | solution.py:43
  103.8 1.1 copy-start.3
  104.9 0.9 copy-start.4
  138.9 32.8 %copy-start.2 = (s32[3]{0:T(128)S(1)}, s32[3]{0:T(128)}, u32[]{:S(2)}) copy-start(s32[3]{0:T(128)} %pad_add_fusion.refs_0_) | copy-start | bytes 40
  138.9 2.6 %collective-permute-start.5 = (bf16[4,16,48,128]{3,2,1,0:T(8,128)(2,1)}, bf16[4,16,48,128]{3,2,1,0:T(8,128)(2,1)S(1)}, u32[]{:S(2)}, u32[]{:S(2)}) collective-permute-start(bf16[4,16,48,128]{3,2,1,0:T(8,128)(2,1)} %get-tuple-element.16), channel_id=1, source_target_pairs={{0,1},{1,0},{2,3},{3,2},{4,5},{5,4},{6,7},{7,6},{8,9},{9,8},{10,11... | collective-permute-start | bytes 2359304 | tf_op jit(solution)/shard_map/ppermute | solution.py:43
  168.2 3.5 %collective-permute-start.6 = (bf16[64,48,128]{2,1,0:T(8,128)(2,1)S(1)}, bf16[64,48,128]{2,1,0:T(8,128)(2,1)S(1)}, u32[]{:S(2)}, u32[]{:S(2)}) collective-permute-start(bf16[64,48,128]{2,1,0:T(8,128)(2,1)S(1)} %all_to_all.15.refs_1_), channel_id=1, source_target_pairs={{0,1},{1,0},{2,3},{3,2},{4,5},{5,4},{6,7},{7,6},{8,9},{9,8},{10,11... | collective-permute-start | bytes 2359304 | tf_op jit(solution)/shard_map/ppermute | solution.py:43
where the time goes:
time: 174 us
  Pallas kernels  62 us (36%)
  waiting for transfers between devices  50.7 us (29%)
  starting transfers between devices  30.3 us (17%)
  blocking collectives  25.3 us (15%)
  local copies, waits for them, and re-layouts  3.26 us (2%)
  other arithmetic  2.03 us (1%)
    ppermute x3, waiting for transfers between devices, shift_lat(): return lax.ppermute(x, 'lat', [(i, (i + s) % RING) for i in range(RING)])  46.5 us
    pallas_call x2, Pallas kernels, member(): pl.pallas_call(lambda *refs: member_kernel(*refs, first=first, final=fina...  33.1 us
    all_to_all x1, blocking collectives, over_all(): return lax.all_to_all(x, LL, split_axis=0, concat_axis=0, tiled=True)  25.3 us
    all_to_all x2, starting transfers between devices, over_all(): return lax.all_to_all(x, LL, split_axis=0, concat_axis=0, tiled=True)  23 us
    pallas_call x1, Pallas kernels, bases(): pl.pallas_call(lambda *refs: basis_kernel(*refs, cols=cols, blocks=blocks...  14 us
    pallas_call x1, Pallas kernels, head(): pl.pallas_call(lambda *refs: head_kernel(*refs, half=half, levels=levels,...  9.27 us
    ppermute x4, waiting for transfers between devices, swap(): return lax.ppermute(x, 'mem', SWAP)  4.22 us
    ppermute x4, starting transfers between devices, swap(): return lax.ppermute(x, 'mem', SWAP)  3.84 us
  transfers between devices with their start and end apart: 9, of which 5 were waited for; matrix products, arithmetic and copies ran while one was open for 1% of the time, Pallas kernels for 22%

commit v1 on v0

--- a/solution.py
+++ b/solution.py
@@ -43,19 +43,25 @@
     return lax.ppermute(x, "mem", SWAP)
 
 
+LEAD = 6
+
+
 def turn_block(blocks, turn, levels):
-    have = blocks[0].shape[0]
-    both = jnp.concatenate([block.reshape(have * levels, 128) for block in blocks], axis=1)
-    if have < 16:
-        both = jnp.concatenate([both, jnp.zeros(((16 - have) * levels, 256), BF)], axis=0)
+    both = jnp.concatenate([block.reshape(16 * levels, 128) for block in blocks], axis=1)
     return jnp.dot(turn, both, preferred_element_type=F32).astype(BF)
 
 
-def turner(levels):
+def turner(levels, mirrored, have):
     size = 16 * levels
     to = lax.broadcasted_iota(jnp.int32, (size, size), 0)
     frm = lax.broadcasted_iota(jnp.int32, (size, size), 1)
-    return jnp.where(frm == (to & 15) * levels + (to >> 4), 1.0, 0.0).astype(BF)
+    within = to & 15
+    taken = jnp.where(mirrored, 15 - within, within)
+    return jnp.where((frm == taken * levels + (to >> 4)) & (within < have), 1.0, 0.0).astype(BF)
+
+
+def turn_start(start, mirrored, cols):
+    return jnp.where(mirrored, LEAD + cols - 15 - start, LEAD + start)
 
 
 def head_kernel(place, fields, row_hbm, col_hbm, level_hbm, value_hbm, out, *scratch, half, levels, cols, padded):
@@ -74,10 +80,20 @@
         fetch(level_hbm, level_ref),
         fetch(value_hbm, value_ref),
     ]
-    arriving = [fetch(fields.at[pl.ds(0, 2), g], fields_in.at[:, g]) for g in range(bands)]
+    arriving = [
+        (
+            fetch(fields.at[pl.ds(0, 2), g], fields_in.at[:, g, pl.ds(LEAD, cols)]),
+            fetch(fields.at[pl.ds(0, 2), g, pl.ds(0, 1)], fields_in.at[:, g, pl.ds(LEAD + cols, 1)]),
+        )
+        for g in range(bands)
+    ]
     mem, lat, lon = place[0], place[1], place[2]
+    mirrored = lon >= place[3]
+    for p in range(2):
+        for g in range(bands):
+            fields_in[p, g, :LEAD] = jnp.zeros((LEAD, levels, 128), BF)
+            fields_in[p, g, LEAD + cols + 1 :] = jnp.zeros((LEAD - 1, levels, 128), BF)
     slots = levels * half
-    col_start = lon * cols + mem * half
     acc[...] = jnp.zeros_like(acc)
     slot_ids = lax.broadcasted_iota(jnp.int32, (slots, 128), 0)
     row_ids = lax.broadcasted_iota(jnp.int32, (128, 128), 0)
@@ -86,7 +102,8 @@
 
     def add_group(g, carry):
         rows = pl.ds(pl.multiple_of(g * 8, 8), 8)
-        within = col_ref[rows, :] - col_start
+        column = col_ref[rows, :] - lon * cols
+        within = jnp.where(mirrored & (column > 0), cols - column, column) - mem * half
         inside = (within >= 0) & (within < half)
         keys = jnp.where(inside, level_ref[rows, :] * half + within, -1)
         lat_row = row_ref[rows, :] - lat * 128
@@ -115,12 +132,15 @@
     leaving = [
         fetch(innov, out.at[pl.ds(g * levels, levels), pl.ds(2 * padded, half), :]) for g in range(bands)
     ]
-    turn = turner(levels)
+    turn = turner(levels, mirrored, 16)
+    last_turn = turner(levels, mirrored, cols % 16)
     for g in range(bands):
-        arriving[g].wait()
+        for copy in arriving[g]:
+            copy.wait()
         for start in range(0, padded, 16):
-            have = min(16, cols - start)
-            turned = turn_block([fields_in[p, g, start : start + have] for p in range(2)], turn, levels)
+            rows = pl.ds(turn_start(start, mirrored, cols), 16)
+            matrix = turn if start + 16 <= cols else last_turn
+            turned = turn_block([fields_in[p, g, rows] for p in range(2)], matrix, levels)
             for l in range(levels):
                 for p in range(2):
                     piece = turned[16 * l : 16 * l + 16, 128 * p : 128 * p + 128]
@@ -147,7 +167,7 @@
         out_specs=hbm,
         scratch_shapes=[pltpu.VMEM(array.shape, array.dtype) for array in observed]
         + [
-            pltpu.VMEM((2, bands, cols, levels, lanes), BF),
+            pltpu.VMEM((2, bands, cols + 2 * LEAD, levels, lanes), BF),
             pltpu.VMEM((bands * levels, 2 * padded, lanes), BF),
             pltpu.VMEM((levels, half, lanes), BF),
             pltpu.VMEM((levels * half, 2 * lanes), F32),
@@ -159,28 +179,37 @@
     )(place, fields, *observed)
 
 
-def relayout_last_kernel(in_ref, out_ref, *, cols, levels, padded):
-    turn = turner(levels)
+def relayout_last_kernel(place, in_ref, out_ref, room, *, cols, levels, padded):
+    mirrored = place[2] >= place[3]
+    for p in range(2):
+        room[p, :LEAD] = jnp.zeros((LEAD, levels, 128), BF)
+        room[p, LEAD : LEAD + cols] = in_ref[0, p]
+        room[p, LEAD + cols] = in_ref[0, p, 0]
+        room[p, LEAD + cols + 1 :] = jnp.zeros((LEAD - 1, levels, 128), BF)
+    turn = turner(levels, mirrored, 16)
+    last_turn = turner(levels, mirrored, cols % 16)
     for start in range(0, padded, 16):
-        have = min(16, cols - start)
-        turned = turn_block([in_ref[0, p, start : start + have] for p in range(2)], turn, levels)
+        rows = pl.ds(turn_start(start, mirrored, cols), 16)
+        matrix = turn if start + 16 <= cols else last_turn
+        turned = turn_block([room[p, rows] for p in range(2)], matrix, levels)
         for l in range(levels):
             for p in range(2):
                 piece = turned[16 * l : 16 * l + 16, 128 * p : 128 * p + 128]
                 out_ref[p * levels + l, start : start + 16, :] = piece
 
 
-def relayout_last(fields, padded):
+def relayout_last(place, fields, padded):
     rounds, bands, cols, levels, lanes = fields.shape
     return pl.pallas_call(
-        lambda i, o: relayout_last_kernel(i, o, cols=cols, levels=levels, padded=padded),
+        lambda *refs: relayout_last_kernel(*refs, cols=cols, levels=levels, padded=padded),
         grid=(bands // 2,),
-        in_specs=[pl.BlockSpec((1, 2, cols, levels, lanes), lambda g: (rounds - 1, g, 0, 0, 0))],
+        in_specs=[sspec(), pl.BlockSpec((1, 2, cols, levels, lanes), lambda g: (rounds - 1, g, 0, 0, 0))],
         out_specs=pl.BlockSpec((2 * levels, padded, lanes), lambda g: (g, 0, 0)),
         out_shape=jax.ShapeDtypeStruct((bands * levels, padded, lanes), BF),
+        scratch_shapes=[pltpu.VMEM((2, cols + 2 * LEAD, levels, lanes), BF)],
         compiler_params=params(58),
         name="relayout_last",
-    )(fields)
+    )(place, fields)
 
 
 def turn_cos(turns):
@@ -194,8 +223,8 @@
 
 def basis_kernel(lon_ref, lon_t_ref, lat_ref, lat_t_ref, *, cols, blocks, padded):
     total = cols * blocks
-    half = total // 2
-    tiles = lon_ref.shape[1] // 128
+    nyquist = total // 2
+    width = lon_ref.shape[1] // 2
     lanes = lax.broadcasted_iota(jnp.int32, (padded, 128), 1)
 
     def turns_of(product):
@@ -204,35 +233,32 @@
 
     def lon_rows(j, carry):
         within = lax.broadcasted_iota(jnp.int32, (padded, 128), 0)
-        x = within + cols * j
+        x = jnp.where(within < cols, within + cols * j, cols * (blocks - 1 - j))
         fine = turns_of(x * lanes)
         coarse = turns_of(x * (lanes * 128))
         fine_cos = turn_cos(fine)
         fine_sin = turn_cos(fine - 0.25)
-        scale = jnp.where(within < cols, math.sqrt(2.0 / total), 0.0)
+        scale = jnp.where(within <= cols, math.sqrt(2.0 / total), 0.0)
         coarse_cos = turn_cos(coarse) * scale
         coarse_sin = turn_cos(coarse - 0.25) * scale
-        sign = jnp.where((x & 1) == 0, 1.0, -1.0)
         rows = pl.ds(pl.multiple_of(j * padded, padded), padded)
-        for t in range(tiles):
+        for t in range(width // 128):
             c = lanes + 128 * t
             cos_t = coarse_cos[:, t : t + 1]
             sin_t = coarse_sin[:, t : t + 1]
-            parts = []
-            if 128 * t <= half:
-                parts.append(fine_cos * cos_t - fine_sin * sin_t)
-            if 128 * t + 127 > half:
-                parts.append((fine_sin * cos_t + fine_cos * sin_t) * sign)
-            value = parts[0] if len(parts) == 1 else jnp.where(c <= half, parts[0], parts[1])
-            if t == 0 or 128 * t <= half < 128 * t + 128:
-                value = jnp.where((c == 0) | (c == half), value * math.sqrt(0.5), value)
-            if 128 * t + 127 >= total:
-                value = jnp.where(c < total, value, 0.0)
-            lon_ref[rows, 128 * t : 128 * t + 128] = value.astype(BF)
+            even = fine_cos * cos_t - fine_sin * sin_t
+            odd = fine_sin * cos_t + fine_cos * sin_t
+            if t == 0 or 128 * t <= nyquist < 128 * t + 128:
+                even = jnp.where((c == 0) | (c == nyquist), even * math.sqrt(0.5), even)
+            if 128 * t + 127 >= nyquist:
+                even = jnp.where(c <= nyquist, even, 0.0)
+                odd = jnp.where(c < nyquist, odd, 0.0)
+            lon_ref[rows, 128 * t : 128 * t + 128] = even.astype(BF)
+            lon_ref[rows, width + 128 * t : width + 128 * t + 128] = odd.astype(BF)
         return carry
 
-    lax.fori_loop(0, blocks, lon_rows, 0)
-    for t in range(tiles):
+    lax.fori_loop(0, blocks // 2, lon_rows, 0)
+    for t in range(lon_ref.shape[1] // 128):
         strip = lon_ref[:, 128 * t : 128 * t + 128].astype(F32)
         lon_t_ref[128 * t : 128 * t + 128, :] = strip.T.astype(BF)
 
@@ -254,12 +280,12 @@
 
 
 def bases(cols, blocks, padded, lat_total):
-    wide = padded * blocks
+    tall = padded * blocks // 2
     return pl.pallas_call(
         lambda *refs: basis_kernel(*refs, cols=cols, blocks=blocks, padded=padded),
         out_shape=(
-            jax.ShapeDtypeStruct((wide, wide), BF),
-            jax.ShapeDtypeStruct((wide, wide), BF),
+            jax.ShapeDtypeStruct((tall, 2 * tall), BF),
+            jax.ShapeDtypeStruct((2 * tall, tall), BF),
             jax.ShapeDtypeStruct((lat_total, lat_total), BF),
             jax.ShapeDtypeStruct((lat_total, lat_total), BF),
         ),
@@ -272,6 +298,8 @@
 
 def arrange_kernel(place, own, other, taper, *, rows_each):
     mem, lat = place[0], place[1]
+    spare = taper.shape[1] - RING * rows_each
+    taper[:, RING * rows_each :, :] = jnp.zeros((4, spare, 128), BF)
     for ref, side in ((own, mem), (other, 1 - mem)):
         for u in range(RING):
             into = pl.ds(pl.multiple_of(lax.rem(lat + RING - u, RING) * rows_each, 8), rows_each)
@@ -283,7 +311,7 @@
     rows_each = own.shape[1]
     return pl.pallas_call(
         lambda *refs: arrange_kernel(*refs, rows_each=rows_each),
-        out_shape=jax.ShapeDtypeStruct((4, RING * rows_each, 128), BF),
+        out_shape=jax.ShapeDtypeStruct((4, RING * rows_each + 32, 128), BF),
         in_specs=[sspec(), vspec(), vspec()],
         out_specs=vspec(),
         compiler_params=params(12),
@@ -297,14 +325,15 @@
     rest = list(refs[9:])
     so_far_hbm = None if first else rest.pop(0)
     outs = [rest.pop(0) for _ in range(2 if final else 1)]
-    weighted, inverse, field, innov, taper, lon_ref, lon_t_ref, lat_ref, lat_t_ref, acc, sems = rest[:11]
+    folded, inverse, field, innov, taper, lon_ref, lon_t_ref, lat_ref, lat_t_ref, acc, sems = rest[:11]
     stages = rest[11:] if final else [acc]
-    wide = padded * blocks
-    parts = 3
-    step = coefs // parts
+    pairs = blocks // 2
+    tall = padded * pairs
+    nyquist = coefs // 2
+    parts = 4
+    step = (nyquist // 2 + 16) // 16 * 16
     group = 4
-    turns = blocks // group
-    tall = group * padded
+    turns = pairs // group
     half = padded // 2
     mem = place[0]
     own_rows = pl.ds(pl.multiple_of(mem * half, half), half)
@@ -314,19 +343,23 @@
         return pltpu.make_async_copy(source, target, sems.at[spot])
 
     def lon_t_copy(r):
-        rows = pl.ds(pl.multiple_of(r * step, 16), step)
+        rows = pl.ds(pl.multiple_of((r // 2) * tall + (r % 2) * step, 16), step)
         return move(lon_t_hbm.at[rows], lon_t_ref.at[rows], 10 + r)
 
     def lon_copy(b):
-        rows = pl.ds(pl.multiple_of(b * tall, tall), tall)
+        rows = pl.ds(pl.multiple_of(b * group * padded, padded), group * padded)
         return move(lon_hbm.at[rows], lon_ref.at[rows], 14 + b)
 
-    def so_far_copy(b):
-        return move(so_far_hbm.at[:, pl.ds(b * group, group)], acc.at[:, pl.ds(b * group, group)], 18 + b)
-
-    def out_copy(b, n):
-        spots = pl.ds(b * group, group)
-        return move(stages[n].at[:, spots], outs[n].at[:, spots], 22 + 4 * n + b)
+    def spots(b, side):
+        return pl.ds((blocks - group - b * group) if side else b * group, group)
+
+    def so_far_copy(b, side):
+        at = spots(b, side)
+        return move(so_far_hbm.at[:, at], acc.at[:, at], 18 + 2 * b + side)
+
+    def out_copy(b, side, n):
+        at = spots(b, side)
+        return move(stages[n].at[:, at], outs[n].at[:, at], 22 + 4 * n + 2 * b + side)
 
     innov_copies = [
         move(pair_hbm.at[:, :, pl.ds(2 * padded, half), :], innov.at[:, :, own_rows, :], 0),
@@ -343,33 +376,47 @@
     ]
     for copy in innov_copies + field_copies + table_copies:
         copy.start()
-    inverse[coefs:, :] = jnp.zeros((wide - coefs, inverse.shape[1]), BF)
+    for side in range(2):
+        inverse[side, 2 * step :, :] = jnp.zeros((tall - 2 * step, inverse.shape[2]), BF)
     for copy in innov_copies:
         copy.wait()
+    down = lax.broadcasted_iota(jnp.int32, (padded, 128), 0)
+    cols = coefs // blocks
 
     def weigh(i, a):
+        def product(j):
+            return field[a, j, i * padded : (i + 1) * padded, :].astype(F32) * innov[a, j].astype(F32)
+
         def body(j, carry):
             rows = pl.ds(pl.multiple_of(j * padded, padded), padded)
-            product = field[a, j, i * padded : (i + 1) * padded, :] * innov[a, j]
-            weighted[rows, 128 * a : 128 * a + 128] = product
+            near = product(j)
+            far = product(blocks - 1 - j)
+            near = jnp.where(down == cols, far[0:1, :], near)
+            far = jnp.where(down == 0, 0.0, far)
+            folded[0, rows, 128 * a : 128 * a + 128] = (near + far).astype(BF)
+            folded[1, rows, 128 * a : 128 * a + 128] = (near - far).astype(BF)
             return carry
 
-        lax.fori_loop(0, blocks, body, 0)
+        lax.fori_loop(0, pairs, body, 0)
 
     def spectral(fresh):
         def body(r, carry):
-            rows = pl.ds(pl.multiple_of(r * step, 16), step)
+            side = r // 2
+            rows = pl.ds(pl.multiple_of((r % 2) * step, 16), step)
+            table = pl.ds(pl.multiple_of(side * tall + (r % 2) * step, 16), step)
+            weight_rows = pl.ds(pl.multiple_of(side * nyquist + (r % 2) * step, 16), step)
             if fresh:
 
                 @pl.when(r > 0)
                 def _():
                     lon_t_copy(r).wait()
 
-            zonal = jnp.dot(lon_t_ref[rows, :], weighted[...], preferred_element_type=F32).astype(BF)
+            zonal = jnp.dot(lon_t_ref[table, :], folded[side], preferred_element_type=F32).astype(BF)
             spectrum = jnp.dot(zonal, lat_ref[...], preferred_element_type=F32)
-            weights = jnp.concatenate([taper[q, rows, :] for q in range(4)], axis=1).astype(F32)
+            weights = jnp.concatenate([taper[q, weight_rows, :] for q in range(4)], axis=1).astype(F32)
             tapered = (spectrum * weights).astype(BF)
-            inverse[rows, :] = jnp.dot(tapered, lat_t_ref[...], preferred_element_type=F32).astype(BF)
+            back = jnp.dot(tapered, lat_t_ref[...], preferred_element_type=F32).astype(BF)
+            inverse[side, rows, :] = back
             if fresh:
 
                 @pl.when(r == 0)
@@ -377,7 +424,8 @@
                     for b in range(turns):
                         lon_copy(b).start()
                         if not first:
-                            so_far_copy(b).start()
+                            so_far_copy(b, 0).start()
+                            so_far_copy(b, 1).start()
 
             return carry
 
@@ -385,27 +433,37 @@
 
     def gridded(i):
         def body(b, carry):
-            rows = pl.ds(pl.multiple_of(b * tall, tall), tall)
+            rows = pl.ds(pl.multiple_of(b * group * padded, padded), group * padded)
             if i == 0:
                 lon_copy(b).wait()
                 if not first:
-                    so_far_copy(b).wait()
-            localized = jnp.dot(lon_ref[rows, :], inverse[...], preferred_element_type=F32)
+                    so_far_copy(b, 0).wait()
+                    so_far_copy(b, 1).wait()
+            even = jnp.dot(lon_ref[rows, :tall], inverse[0], preferred_element_type=F32)
+            odd = jnp.dot(lon_ref[rows, tall:], inverse[1], preferred_element_type=F32)
+
+            def put(piece, a, j):
+                piece = piece * field[a, j, i * padded : (i + 1) * padded, :].astype(F32)
+                piece = piece if first and i == 0 else piece + acc[a, j]
+                if final:
+                    top, low = piece[:half], piece[half:]
+                    stages[0][a, j] = jnp.where(mem == 0, top, low).astype(BF)
+                    stages[1][a, j] = jnp.where(mem == 0, low, top).astype(BF)
+                else:
+                    acc[a, j] = piece
+
             for g in range(group):
                 for a in range(bands):
                     j = b * group + g
-                    piece = localized[g * padded : (g + 1) * padded, 128 * a : 128 * a + 128]
-                    piece = piece * field[a, j, i * padded : (i + 1) * padded, :].astype(F32)
-                    piece = piece if first and i == 0 else piece + acc[a, j]
-                    if final:
-                        top, low = piece[:half], piece[half:]
-                        stages[0][a, j] = jnp.where(mem == 0, top, low).astype(BF)
-                        stages[1][a, j] = jnp.where(mem == 0, low, top).astype(BF)
-                    else:
-                        acc[a, j] = piece
+                    spot = (slice(g * padded, (g + 1) * padded), slice(128 * a, 128 * a + 128))
+                    near = even[spot] + odd[spot]
+                    far = jnp.where(down == 0, near[cols : cols + 1, :], even[spot] - odd[spot])
+                    put(near, a, j)
+                    put(far, a, blocks - 1 - j)
             if i == count - 1:
                 for n in range(len(outs)):
-                    out_copy(b, n).start()
+                    out_copy(b, 0, n).start()
+                    out_copy(b, 1, n).start()
             return carry
 
         lax.fori_loop(0, turns, body, 0)
@@ -424,19 +482,20 @@
         gridded(i)
     for b in range(turns):
         for n in range(len(outs)):
-            out_copy(b, n).wait()
+            out_copy(b, 0, n).wait()
+            out_copy(b, 1, n).wait()
 
 
 def member(place, field, pair, other, taper, tables, so_far, final, dims):
     _, blocks, bands, padded, coefs, lat_total = dims
     half = padded // 2
-    wide = padded * blocks
+    tall = padded * blocks // 2
     first = so_far is None
     count = 1 if final else 2
     split = lambda array: array.reshape(bands, blocks, *array.shape[1:])
     far = [split(field), split(pair), split(other), taper, *tables] + ([] if first else [so_far])
     block = lambda rows, dtype: ((bands, blocks, rows, 128), dtype)
-    scratch = [((wide, lat_total), BF), ((wide, lat_total), BF), block(count * padded, BF), block(padded, BF)]
+    scratch = [((2, tall, lat_total), BF), ((2, tall, lat_total), BF), block(count * padded, BF), block(padded, BF)]
     scratch += [(array.shape, array.dtype) for array in (taper, *tables)]
     scratch.append(block(padded, F32))
     results = [block(half, BF), block(half, BF)] if final else [block(padded, F32)]
@@ -459,14 +518,20 @@
 
 def finish_kernel(place, own, other, out, *, levels, cols, half, scale):
     mem = place[0]
+    mirrored = place[2] >= place[3]
     bands = own.shape[0] // levels
-    for side in range(2):
-        rows = min(half, cols - side * half)
-        for l in range(levels):
-            mine = sum(own[a * levels + l].astype(F32) for a in range(bands))
-            theirs = sum(other[a * levels + l].astype(F32) for a in range(bands))
-            total = jnp.where(mem == side, mine, theirs) * scale
-            out[side * half : side * half + rows, l, :] = total[:rows]
+    to = lax.broadcasted_iota(jnp.int32, (2 * half, half), 0)
+    frm = lax.broadcasted_iota(jnp.int32, (2 * half, half), 1)
+    taken = jnp.where(mirrored & (to > 0), cols - to, to)
+    picks = [jnp.where(taken == frm + side * half, 1.0, 0.0).astype(BF) for side in (mem, 1 - mem)]
+    picks = jnp.concatenate(picks * bands, axis=1)
+    columns = []
+    for l in range(levels):
+        parts = [ref[a * levels + l] for a in range(bands) for ref in (own, other)]
+        columns.append(jnp.concatenate(parts, axis=0))
+    summed = jnp.dot(picks, jnp.concatenate(columns, axis=1), preferred_element_type=F32) * scale
+    for l in range(levels):
+        out[:, l, :] = summed[:cols, 128 * l : 128 * l + 128]
 
 
 def finish(place, own, other, levels, cols, half, scale):
@@ -475,7 +540,7 @@
         out_shape=jax.ShapeDtypeStruct((cols, levels, 128), F32),
         in_specs=[sspec(), vspec(), vspec()],
         out_specs=vspec(),
-        compiler_params=params(12),
+        compiler_params=params(16),
         name="finish",
     )(place, own, other)
 
@@ -490,7 +555,7 @@
     padded = -(-cols // 32) * 32
     half = padded // 2
     ensemble = members * lax.axis_size("mem")
-    place = jnp.stack([mem, lat, lon]).astype(jnp.int32)
+    place = jnp.stack([mem, lat, lon, jnp.int32(blocks // 2)]).astype(jnp.int32)
 
     by_round = jnp.transpose(anomalies, (0, 2, 1, 3)).reshape(members // bands, bands, cols, levels, lat_rows)
     pair_out = head(place, by_round, obs_row, obs_col, obs_level, obs_value, half, padded)
@@ -500,7 +565,7 @@
     ring = [taper_mine]
     for u in range(1, RING):
         ring.append(shift_lat(taper_mine, u))
-    last_out = relayout_last(by_round, padded)
+    last_out = relayout_last(place, by_round, padded)
     last = over_all(last_out)
     own = jnp.stack(ring)
     weights = arrange(place, own, swap(own))

time: 174 us -> 162 us (0.931)
  Pallas kernels: 62 us -> 50.1 us
    pallas_call x1, Pallas kernels: 14 us -> 7.02 us  [bases(): pl.pallas_call(lambda *refs: basis_kernel(*refs, cols=cols, blocks=blocks...]
    pallas_call x2, Pallas kernels: 33.1 us -> 27.8 us  [member(): pl.pallas_call(lambda *refs: member_kernel(*refs, first=first, final=fina...]
  transfers between devices with their start and end apart: 9 -> 9, of which waited for: 5 -> 5; matrix products, arithmetic and copies ran while one was open for 1% -> 1% of each run, Pallas kernels for 22% -> 17%
where the time goes in v1:
time: 162 us
  waiting for transfers between devices  50.5 us (31%)
  Pallas kernels  50.1 us (31%)
  starting transfers between devices  30.4 us (19%)
  blocking collectives  25.4 us (16%)
  local copies, waits for them, and re-layouts  3.32 us (2%)
  other arithmetic  2.11 us (1%)
    ppermute x3, waiting for transfers between devices, shift_lat(): return lax.ppermute(x, 'lat', [(i, (i + s) % RING) for i in range(RING)])  46.3 us
    pallas_call x2, Pallas kernels, member(): pl.pallas_call(lambda *refs: member_kernel(*refs, first=first, final=fina...  27.8 us
    all_to_all x1, blocking collectives, over_all(): return lax.all_to_all(x, LL, split_axis=0, concat_axis=0, tiled=True)  25.4 us
    all_to_all x2, starting transfers between devices, over_all(): return lax.all_to_all(x, LL, split_axis=0, concat_axis=0, tiled=True)  23 us
    pallas_call x1, Pallas kernels, head(): pl.pallas_call(lambda *refs: head_kernel(*refs, half=half, levels=levels,...  9.38 us
    pallas_call x1, Pallas kernels, bases(): pl.pallas_call(lambda *refs: basis_kernel(*refs, cols=cols, blocks=blocks...  7.02 us
    ppermute x4, waiting for transfers between devices, swap(): return lax.ppermute(x, 'mem', SWAP)  4.2 us
    ppermute x4, starting transfers between devices, swap(): return lax.ppermute(x, 'mem', SWAP)  3.86 us
  transfers between devices with their start and end apart: 9, of which 5 were waited for; matrix products, arithmetic and copies ran while one was open for 1% of the time, Pallas kernels for 17%

profile of v1, /device:TPU:1, one launch (start us, length us, event | category | flops | bytes accessed | tf_op | source)
XLA Modules:
  0.0 161.9 jit_solution(624823677048123450)
XLA Ops:
  0.0 0.0 copy-start
  0.0 0.7 pad_add_fusion.refs_0_
  0.7 9.4 %head.1 = bf16[64,240,128]{2,1,0:T(8,128)(2,1)} custom-call(s32[4]{0:T(128)} %pad_add_fusion.refs_0_, bf16[3,4,90,16,128]{4,3,2,1,0:T(8,128)(2,1)} %bitcast.16, s32[64,128]{1,0:T(8,128)} %refs_2_.1, s32[64,128]{1,0:T(8,128)} %refs_3_.1, s32[64,128]{1,0:T(8,128)} %refs_4_.1, f32[64,128]{1,0:T(8,128)} %refs_5_.1), custom_call_target="tpu_custom_call" | custom-call | flops 6000000000 | bytes 1048576 | tf_op jit(solution)/shard_map/head/pallas_call | solution.py:163
  10.1 12.2 %all-to-all-start.1 = ((bf16[64,240,128]{2,1,0:T(8,128)(2,1)}), bf16[64,240,128]{2,1,0:T(8,128)(2,1)}, u32[]{:S(2)}, u32[]{:S(2)}) async-start(bf16[64,240,128]{2,1,0:T(8,128)(2,1)} %head.1), calls=%async_computation.1 | async-start | bytes 7864320 | tf_op jit(solution)/shard_map/all_to_all | solution.py:35
  22.3 0.0 copy-done
  22.3 2.4 %collective-permute-start.3 = (bf16[360,256]{1,0:T(8,128)(2,1)S(1)}, bf16[360,256]{1,0:T(8,128)(2,1)S(1)}, u32[]{:S(2)}, u32[]{:S(2)}) collective-permute-start(bf16[360,256]{1,0:T(8,128)(2,1)S(1)} %fusion), channel_id=1, source_target_pairs={{0,96},{32,0},{64,32},{96,64},{1,97},{33,1},{65,33},{97,65},{2,98}... | collective-permute-start | bytes 552968 | tf_op jit(solution)/shard_map/ppermute | solution.py:39
  24.8 0.4 collective-permute-start.2
  25.1 0.7 collective-permute-start.1
  25.8 2.9 %relayout_last.1 = bf16[64,96,128]{2,1,0:T(8,128)(2,1)} custom-call(s32[4]{0:T(128)} %pad_add_fusion.refs_0_, bf16[3,4,90,16,128]{4,3,2,1,0:T(8,128)(2,1)} %bitcast.17), custom_call_target="tpu_custom_call" | custom-call | tf_op jit(solution)/shard_map/relayout_last/pallas_call | solution.py:203
  28.8 40.8 %collective-permute-done.3 = bf16[360,256]{1,0:T(8,128)(2,1)S(1)} collective-permute-done((bf16[360,256]{1,0:T(8,128)(2,1)S(1)}, bf16[360,256]{1,0:T(8,128)(2,1)S(1)}, u32[]{:S(2)}, u32[]{:S(2)}) %collective-permute-start.3) | collective-permute-done | bytes 184352 | tf_op jit(solution)/shard_map/ppermute | solution.py:39
  69.6 2.2 %collective-permute-done.2 = bf16[360,256]{1,0:T(8,128)(2,1)S(1)} collective-permute-done((bf16[360,256]{1,0:T(8,128)(2,1)S(1)}, bf16[360,256]{1,0:T(8,128)(2,1)S(1)}, u32[]{:S(2)}, u32[]{:S(2)}) %collective-permute-start.2) | collective-permute-done | bytes 184352 | tf_op jit(solution)/shard_map/ppermute | solution.py:39
  71.8 3.3 %collective-permute-done.1 = bf16[360,256]{1,0:T(8,128)(2,1)S(1)} collective-permute-done((bf16[360,256]{1,0:T(8,128)(2,1)S(1)}, bf16[360,256]{1,0:T(8,128)(2,1)S(1)}, u32[]{:S(2)}, u32[]{:S(2)}) %collective-permute-start.1) | collective-permute-done | bytes 184352 | tf_op jit(solution)/shard_map/ppermute | solution.py:39
  75.1 0.1 pad_maximum_fusion.refs_1_
  75.2 1.4 collective-permute-start.4
  76.6 0.0 all-to-all-done.1
  76.6 10.8 %all-to-all-start = ((bf16[64,96,128]{2,1,0:T(8,128)(2,1)}), bf16[64,96,128]{2,1,0:T(8,128)(2,1)}, u32[]{:S(2)}, u32[]{:S(2)}) async-start(bf16[64,96,128]{2,1,0:T(8,128)(2,1)} %relayout_last.1), calls=%async_computation | async-start | bytes 3145728 | tf_op jit(solution)/shard_map/all_to_all | solution.py:35
  87.4 1.2 slice.4
  88.6 0.0 copy-start.1
  88.6 0.6 collective-permute-start
  89.2 7.0 %bases.1 = (bf16[768,1536]{1,0:T(8,128)(2,1)}, bf16[1536,768]{1,0:T(8,128)(2,1)}, bf16[512,512]{1,0:T(8,128)(2,1)}, bf16[512,512]{1,0:T(8,128)(2,1)}) custom-call(), custom_call_target="tpu_custom_call" | custom-call | flops 12000000000 | bytes 1048576 | tf_op jit(solution)/shard_map/bases/pallas_call | solution.py:284
  96.2 0.0 collective-permute-done.4.refs_2_
  96.2 0.0 copy-done.1
  96.2 0.8 arrange.1.refs_4_
  97.0 0.0 copy-start.3
  97.0 1.2 copy-done.3
  98.2 0.0 collective-permute-done
  98.2 0.0 copy-start.4
  98.2 0.9 copy-done.4
  99.1 17.4 %member_pair.1.refs_9_ = f32[4,16,96,128]{3,2,1,0:T(8,128)} custom-call(s32[4]{0:T(128)} %pad_add_fusion.refs_0_, bf16[4,16,240,128]{3,2,1,0:T(8,128)(2,1)} %bitcast.7.refs_1_.refs_2_, bf16[4,16,240,128]{3,2,1,0:T(8,128)(2,1)} %bitcast.7.refs_1_.refs_2_, bf16[4,16,48,128]{3,2,1,0:T(8,128)(2,1)} %bitcast.22, bf16[4,1472,128]{2,1,0:T(8,128)(2,1)} %copy-done.3, ...), custom_call_target="tpu_custom_call" | custom-call | flops 12000000000 | bytes 1048576 | tf_op jit(solution)/shard_map/member_pair/pallas_call | solution.py:503
  116.5 0.0 all-to-all-done
  116.5 10.4 %member_last.1 = (bf16[4,16,48,128]{3,2,1,0:T(8,128)(2,1)}, bf16[4,16,48,128]{3,2,1,0:T(8,128)(2,1)}) custom-call(s32[4]{0:T(128)} %pad_add_fusion.refs_0_, bf16[4,16,96,128]{3,2,1,0:T(8,128)(2,1)} %bitcast.5.refs_1_, bf16[4,16,240,128]{3,2,1,0:T(8,128)(2,1)} %bitcast.7.refs_1_.refs_2_, bf16[4,16,48,128]{3,2,1,0:T(8,128)(2,1)} %bitcast.23, ...), custom_call_target="tpu_custom_call" | custom-call | flops 6000000000 | bytes 1048576 | tf_op jit(solution)/shard_map/member_last/pallas_call | solution.py:503
  126.9 0.0 copy-start.2
  127.0 0.3 collective-permute-start.5
  127.2 2.3 %collective-permute-done.5 = bf16[4,16,48,128]{3,2,1,0:T(8,128)(2,1)S(1)} collective-permute-done((bf16[4,16,48,128]{3,2,1,0:T(8,128)(2,1)}, bf16[4,16,48,128]{3,2,1,0:T(8,128)(2,1)S(1)}, u32[]{:S(2)}, u32[]{:S(2)}) %collective-permute-start.5) | collective-permute-done | bytes 786464 | tf_op jit(solution)/shard_map/ppermute | solution.py:43
  129.5 1.3 add_convert_fusion
  130.9 25.4 %all_to_all.15.refs_1_ = bf16[64,48,128]{2,1,0:T(8,128)(2,1)S(1)} all-to-all(bf16[64,48,128]{2,1,0:T(8,128)(2,1)S(1)} %bitcast.18), channel_id=1, replica_groups=mesh['lat'=4,'lon'=16,'mem'=2] {'lat','lon'}, dimensions={0} | all-to-all | bytes 1572864 | tf_op jit(solution)/shard_map/all_to_all | solution.py:35
  156.3 1.6 collective-permute-start.6
  157.8 1.9 %collective-permute-done.6.refs_2_ = bf16[64,48,128]{2,1,0:T(8,128)(2,1)S(1)} collective-permute-done((bf16[64,48,128]{2,1,0:T(8,128)(2,1)S(1)}, bf16[64,48,128]{2,1,0:T(8,128)(2,1)S(1)}, u32[]{:S(2)}, u32[]{:S(2)}) %collective-permute-start.6) | collective-permute-done | bytes 786464 | tf_op jit(solution)/shard_map/ppermute | solution.py:43
  159.8 0.0 copy-done.2
  159.8 2.1 %finish.1 = f32[90,16,128]{2,1,0:T(8,128)} custom-call(s32[4]{0:T(128)S(1)} %copy-done.2, bf16[64,48,128]{2,1,0:T(8,128)(2,1)S(1)} %all_to_all.15.refs_1_, bf16[64,48,128]{2,1,0:T(8,128)(2,1)S(1)} %collective-permute-done.6.refs_2_), custom_call_target="tpu_custom_call" | custom-call | tf_op jit(solution)/shard_map/finish/pallas_call | solution.py:538
  (2 shorter events, 0.1 us)
Async XLA Ops:
  0.0 22.3 %copy-start = (f32[1,360,512]{2,1,0:T(8,128)S(1)}, f32[1,360,512]{2,1,0:T(8,128)}, u32[]{:S(2)}) copy-start(f32[1,360,512]{2,1,0:T(8,128)} %param.7) | copy-start | bytes 2211844
  10.1 66.5 %all-to-all-start.1 = ((bf16[64,240,128]{2,1,0:T(8,128)(2,1)}), bf16[64,240,128]{2,1,0:T(8,128)(2,1)}, u32[]{:S(2)}, u32[]{:S(2)}) async-start(bf16[64,240,128]{2,1,0:T(8,128)(2,1)} %head.1), calls=%async_computation.1 | async-start | bytes 7864320 | tf_op jit(solution)/shard_map/all_to_all | solution.py:35
  22.3 47.3 %collective-permute-start.3 = (bf16[360,256]{1,0:T(8,128)(2,1)S(1)}, bf16[360,256]{1,0:T(8,128)(2,1)S(1)}, u32[]{:S(2)}, u32[]{:S(2)}) collective-permute-start(bf16[360,256]{1,0:T(8,128)(2,1)S(1)} %fusion), channel_id=1, source_target_pairs={{0,96},{32,0},{64,32},{96,64},{1,97},{33,1},{65,33},{97,65},{2,98}... | collective-permute-start | bytes 552968 | tf_op jit(solution)/shard_map/ppermute | solution.py:39
  24.8 47.1 %collective-permute-start.2 = (bf16[360,256]{1,0:T(8,128)(2,1)S(1)}, bf16[360,256]{1,0:T(8,128)(2,1)S(1)}, u32[]{:S(2)}, u32[]{:S(2)}) collective-permute-start(bf16[360,256]{1,0:T(8,128)(2,1)S(1)} %fusion), channel_id=1, source_target_pairs={{0,64},{32,96},{64,0},{96,32},{1,65},{33,97},{65,1},{97,33},{2,66}... | collective-permute-start | bytes 552968 | tf_op jit(solution)/shard_map/ppermute | solution.py:39
  25.1 49.9 %collective-permute-start.1 = (bf16[360,256]{1,0:T(8,128)(2,1)S(1)}, bf16[360,256]{1,0:T(8,128)(2,1)S(1)}, u32[]{:S(2)}, u32[]{:S(2)}) collective-permute-start(bf16[360,256]{1,0:T(8,128)(2,1)S(1)} %fusion), channel_id=1, source_target_pairs={{0,32},{32,64},{64,96},{96,0},{1,33},{33,65},{65,97},{97,1},{2,34}... | collective-permute-start | bytes 552968 | tf_op jit(solution)/shard_map/ppermute | solution.py:39
  75.2 21.1 %collective-permute-start.4 = (bf16[4,360,256]{2,1,0:T(8,128)(2,1)S(1)}, bf16[4,360,256]{2,1,0:T(8,128)(2,1)S(1)}, u32[]{:S(2)}, u32[]{:S(2)}) collective-permute-start(bf16[4,360,256]{2,1,0:T(8,128)(2,1)S(1)} %pad_maximum_fusion.refs_1_), channel_id=1, source_target_pairs={{0,1},{1,0},{2,3},{3,2},{4,5},{5,4},{6,7},{7,6},{8,9},{9,8},{10,11... | collective-permute-start | bytes 2211848 | tf_op jit(solution)/shard_map/ppermute | solution.py:43
  76.6 39.9 %all-to-all-start = ((bf16[64,96,128]{2,1,0:T(8,128)(2,1)}), bf16[64,96,128]{2,1,0:T(8,128)(2,1)}, u32[]{:S(2)}, u32[]{:S(2)}) async-start(bf16[64,96,128]{2,1,0:T(8,128)(2,1)} %relayout_last.1), calls=%async_computation | async-start | bytes 3145728 | tf_op jit(solution)/shard_map/all_to_all | solution.py:35
  88.6 7.6 %copy-start.1 = (s32[4]{0:T(128)S(1)}, s32[4]{0:T(128)}, u32[]{:S(2)}) copy-start(s32[4]{0:T(128)} %pad_add_fusion.refs_0_) | copy-start | bytes 52
  88.6 9.6 %collective-permute-start = (bf16[64,48,128]{2,1,0:T(8,128)(2,1)S(1)}, bf16[64,48,128]{2,1,0:T(8,128)(2,1)S(1)}, u32[]{:S(2)}, u32[]{:S(2)}) collective-permute-start(bf16[64,48,128]{2,1,0:T(8,128)(2,1)S(1)} %slice.4), channel_id=1, source_target_pairs={{0,1},{1,0},{2,3},{3,2},{4,5},{5,4},{6,7},{7,6},{8,9},{9,8},{10,11... | collective-permute-start | bytes 2359304 | tf_op jit(solution)/shard_map/ppermute | solution.py:43
  97.0 1.2 copy-start.3
  98.2 0.9 copy-start.4
  126.9 32.8 %copy-start.2 = (s32[4]{0:T(128)S(1)}, s32[4]{0:T(128)}, u32[]{:S(2)}) copy-start(s32[4]{0:T(128)} %pad_add_fusion.refs_0_) | copy-start | bytes 52
  127.0 2.6 %collective-permute-start.5 = (bf16[4,16,48,128]{3,2,1,0:T(8,128)(2,1)}, bf16[4,16,48,128]{3,2,1,0:T(8,128)(2,1)S(1)}, u32[]{:S(2)}, u32[]{:S(2)}) collective-permute-start(bf16[4,16,48,128]{3,2,1,0:T(8,128)(2,1)} %get-tuple-element.16), channel_id=1, source_target_pairs={{0,1},{1,0},{2,3},{3,2},{4,5},{5,4},{6,7},{7,6},{8,9},{9,8},{10,11... | collective-permute-start | bytes 2359304 | tf_op jit(solution)/shard_map/ppermute | solution.py:43
  156.3 3.5 %collective-permute-start.6 = (bf16[64,48,128]{2,1,0:T(8,128)(2,1)S(1)}, bf16[64,48,128]{2,1,0:T(8,128)(2,1)S(1)}, u32[]{:S(2)}, u32[]{:S(2)}) collective-permute-start(bf16[64,48,128]{2,1,0:T(8,128)(2,1)S(1)} %all_to_all.15.refs_1_), channel_id=1, source_target_pairs={{0,1},{1,0},{2,3},{3,2},{4,5},{5,4},{6,7},{7,6},{8,9},{9,8},{10,11... | collective-permute-start | bytes 2359304 | tf_op jit(solution)/shard_map/ppermute | solution.py:43

commit v2 on v1

--- a/solution.py
+++ b/solution.py
@@ -326,7 +326,7 @@
     so_far_hbm = None if first else rest.pop(0)
     outs = [rest.pop(0) for _ in range(2 if final else 1)]
     folded, inverse, field, innov, taper, lon_ref, lon_t_ref, lat_ref, lat_t_ref, acc, sems = rest[:11]
-    stages = rest[11:] if final else [acc]
+    stages = rest[11:]
     pairs = blocks // 2
     tall = padded * pairs
     nyquist = coefs // 2
@@ -370,6 +370,7 @@
     ]
     table_copies = [
         lon_t_copy(0),
+        lon_t_copy(2),
         move(lat_hbm, lat_ref, 7),
         move(taper_hbm, taper, 8),
         move(lat_t_hbm, lat_t_ref, 9),
@@ -401,22 +402,28 @@
 
     def spectral(fresh):
         def body(r, carry):
-            side = r // 2
-            rows = pl.ds(pl.multiple_of((r % 2) * step, 16), step)
-            table = pl.ds(pl.multiple_of(side * tall + (r % 2) * step, 16), step)
-            weight_rows = pl.ds(pl.multiple_of(side * nyquist + (r % 2) * step, 16), step)
+            rows = pl.ds(pl.multiple_of(r * step, 16), step)
             if fresh:
 
                 @pl.when(r > 0)
                 def _():
-                    lon_t_copy(r).wait()
-
-            zonal = jnp.dot(lon_t_ref[table, :], folded[side], preferred_element_type=F32).astype(BF)
-            spectrum = jnp.dot(zonal, lat_ref[...], preferred_element_type=F32)
-            weights = jnp.concatenate([taper[q, weight_rows, :] for q in range(4)], axis=1).astype(F32)
-            tapered = (spectrum * weights).astype(BF)
-            back = jnp.dot(tapered, lat_t_ref[...], preferred_element_type=F32).astype(BF)
-            inverse[side, rows, :] = back
+                    for side in range(2):
+                        lon_t_copy(2 * side + r).wait()
+
+            tables = [pl.ds(pl.multiple_of(side * tall + r * step, 16), step) for side in range(2)]
+            zonal = [
+                jnp.dot(lon_t_ref[tables[side], :], folded[side], preferred_element_type=F32).astype(BF)
+                for side in range(2)
+            ]
+            spectrum = [jnp.dot(zonal[side], lat_ref[...], preferred_element_type=F32) for side in range(2)]
+            tapered = []
+            for side in range(2):
+                weight_rows = pl.ds(pl.multiple_of(side * nyquist + r * step, 16), step)
+                weights = jnp.concatenate([taper[q, weight_rows, :] for q in range(4)], axis=1).astype(F32)
+                tapered.append((spectrum[side] * weights).astype(BF))
+            for side in range(2):
+                back = jnp.dot(tapered[side], lat_t_ref[...], preferred_element_type=F32)
+                inverse[side, rows, :] = back.astype(BF)
             if fresh:
 
                 @pl.when(r == 0)
@@ -429,7 +436,7 @@
 
             return carry
 
-        lax.fori_loop(0, parts, body, 0)
+        lax.fori_loop(0, parts // 2, body, 0)
 
     def gridded(i):
         def body(b, carry):
@@ -444,11 +451,13 @@
 
             def put(piece, a, j):
                 piece = piece * field[a, j, i * padded : (i + 1) * padded, :].astype(F32)
-                piece = piece if first and i == 0 else piece + acc[a, j]
+                piece = piece if first and i == 0 else piece + acc[a, j].astype(F32)
                 if final:
                     top, low = piece[:half], piece[half:]
                     stages[0][a, j] = jnp.where(mem == 0, top, low).astype(BF)
                     stages[1][a, j] = jnp.where(mem == 0, low, top).astype(BF)
+                elif i == count - 1:
+                    stages[0][a, j] = piece.astype(BF)
                 else:
                     acc[a, j] = piece
 
@@ -466,7 +475,8 @@
                     out_copy(b, 1, n).start()
             return carry
 
-        lax.fori_loop(0, turns, body, 0)
+        for b in range(turns):
+            body(b, 0)
 
     for i in range(count):
         for a in range(bands):
@@ -474,7 +484,7 @@
                 field_copies[a].wait()
             weigh(i, a)
         if i == 0:
-            for r in range(1, parts):
+            for r in (1, 3):
                 lon_t_copy(r).start()
             for copy in table_copies:
                 copy.wait()
@@ -497,8 +507,8 @@
     block = lambda rows, dtype: ((bands, blocks, rows, 128), dtype)
     scratch = [((2, tall, lat_total), BF), ((2, tall, lat_total), BF), block(count * padded, BF), block(padded, BF)]
     scratch += [(array.shape, array.dtype) for array in (taper, *tables)]
-    scratch.append(block(padded, F32))
-    results = [block(half, BF), block(half, BF)] if final else [block(padded, F32)]
+    scratch.append(block(padded, F32 if first else BF))
+    results = [block(half, BF), block(half, BF)] if final else [block(padded, BF)]
     hbm = pl.BlockSpec(memory_space=pltpu.HBM)
     return pl.pallas_call(
         lambda *refs: member_kernel(
@@ -509,7 +519,7 @@
         out_specs=[hbm] * len(results),
         scratch_shapes=[pltpu.VMEM(*each) for each in scratch]
         + [pltpu.SemaphoreType.DMA((32,))]
-        + ([pltpu.VMEM(*each) for each in results] if final else []),
+        + [pltpu.VMEM(*each) for each in results],
         compiler_params=params(60),
         cost_estimate=cost(count * 6e9),
         name="member_last" if final else "member_pair",

time: 162 us -> 160 us (0.988)
  Pallas kernels: 50.1 us -> 47.6 us
    pallas_call x2, Pallas kernels: 27.8 us -> 25.2 us  [member(): pl.pallas_call(lambda *refs: member_kernel(*refs, first=first, final=fina...]
  transfers between devices with their start and end apart: 9 -> 9, of which waited for: 5 -> 5; matrix products, arithmetic and copies ran while one was open for 1% -> 1% of each run, Pallas kernels for 17% -> 16%
where the time goes in v2:
time: 160 us; the launch traced here: 159 us
  waiting for transfers between devices  50.5 us (32%)
  Pallas kernels  47.6 us (30%)
  starting transfers between devices  30.4 us (19%)
  blocking collectives  25.3 us (16%)
  local copies, waits for them, and re-layouts  3.28 us (2%)
  other arithmetic  2.09 us (1%)
    ppermute x3, waiting for transfers between devices, shift_lat(): return lax.ppermute(x, 'lat', [(i, (i + s) % RING) for i in range(RING)])  46.3 us
    all_to_all x1, blocking collectives, over_all(): return lax.all_to_all(x, LL, split_axis=0, concat_axis=0, tiled=True)  25.3 us
    pallas_call x2, Pallas kernels, member(): pl.pallas_call(lambda *refs: member_kernel(*refs, first=first, final=fina...  25.2 us
    all_to_all x2, starting transfers between devices, over_all(): return lax.all_to_all(x, LL, split_axis=0, concat_axis=0, tiled=True)  23 us
    pallas_call x1, Pallas kernels, head(): pl.pallas_call(lambda *refs: head_kernel(*refs, half=half, levels=levels,...  9.38 us
    pallas_call x1, Pallas kernels, bases(): pl.pallas_call(lambda *refs: basis_kernel(*refs, cols=cols, blocks=blocks...  7.06 us
    ppermute x4, waiting for transfers between devices, swap(): return lax.ppermute(x, 'mem', SWAP)  4.21 us
    ppermute x4, starting transfers between devices, swap(): return lax.ppermute(x, 'mem', SWAP)  3.84 us
  transfers between devices with their start and end apart: 9, of which 5 were waited for; matrix products, arithmetic and copies ran while one was open for 1% of the time, Pallas kernels for 16%

profile of v2, /device:TPU:1, one launch (start us, length us, event | category | flops | bytes accessed | tf_op | source)
XLA Modules:
  0.0 159.3 jit_solution(10361208921724477157)
XLA Ops:
  0.0 0.0 copy-start
  0.0 0.7 pad_add_fusion.refs_0_
  0.7 9.4 %head.1 = bf16[64,240,128]{2,1,0:T(8,128)(2,1)} custom-call(s32[4]{0:T(128)} %pad_add_fusion.refs_0_, bf16[3,4,90,16,128]{4,3,2,1,0:T(8,128)(2,1)} %bitcast.16, s32[64,128]{1,0:T(8,128)} %refs_2_.1, s32[64,128]{1,0:T(8,128)} %refs_3_.1, s32[64,128]{1,0:T(8,128)} %refs_4_.1, f32[64,128]{1,0:T(8,128)} %refs_5_.1), custom_call_target="tpu_custom_call" | custom-call | flops 6000000000 | bytes 1048576 | tf_op jit(solution)/shard_map/head/pallas_call | solution.py:163
  10.0 12.2 %all-to-all-start.1 = ((bf16[64,240,128]{2,1,0:T(8,128)(2,1)}), bf16[64,240,128]{2,1,0:T(8,128)(2,1)}, u32[]{:S(2)}, u32[]{:S(2)}) async-start(bf16[64,240,128]{2,1,0:T(8,128)(2,1)} %head.1), calls=%async_computation.1 | async-start | bytes 7864320 | tf_op jit(solution)/shard_map/all_to_all | solution.py:35
  22.3 0.0 copy-done
  22.3 2.4 %collective-permute-start.3 = (bf16[360,256]{1,0:T(8,128)(2,1)S(1)}, bf16[360,256]{1,0:T(8,128)(2,1)S(1)}, u32[]{:S(2)}, u32[]{:S(2)}) collective-permute-start(bf16[360,256]{1,0:T(8,128)(2,1)S(1)} %fusion), channel_id=1, source_target_pairs={{0,96},{32,0},{64,32},{96,64},{1,97},{33,1},{65,33},{97,65},{2,98}... | collective-permute-start | bytes 552968 | tf_op jit(solution)/shard_map/ppermute | solution.py:39
  24.7 0.4 collective-permute-start.2
  25.1 0.7 collective-permute-start.1
  25.8 3.0 %relayout_last.1 = bf16[64,96,128]{2,1,0:T(8,128)(2,1)} custom-call(s32[4]{0:T(128)} %pad_add_fusion.refs_0_, bf16[3,4,90,16,128]{4,3,2,1,0:T(8,128)(2,1)} %bitcast.17), custom_call_target="tpu_custom_call" | custom-call | tf_op jit(solution)/shard_map/relayout_last/pallas_call | solution.py:203
  28.8 40.8 %collective-permute-done.3 = bf16[360,256]{1,0:T(8,128)(2,1)S(1)} collective-permute-done((bf16[360,256]{1,0:T(8,128)(2,1)S(1)}, bf16[360,256]{1,0:T(8,128)(2,1)S(1)}, u32[]{:S(2)}, u32[]{:S(2)}) %collective-permute-start.3) | collective-permute-done | bytes 184352 | tf_op jit(solution)/shard_map/ppermute | solution.py:39
  69.6 2.2 %collective-permute-done.2 = bf16[360,256]{1,0:T(8,128)(2,1)S(1)} collective-permute-done((bf16[360,256]{1,0:T(8,128)(2,1)S(1)}, bf16[360,256]{1,0:T(8,128)(2,1)S(1)}, u32[]{:S(2)}, u32[]{:S(2)}) %collective-permute-start.2) | collective-permute-done | bytes 184352 | tf_op jit(solution)/shard_map/ppermute | solution.py:39
  71.8 3.3 %collective-permute-done.1 = bf16[360,256]{1,0:T(8,128)(2,1)S(1)} collective-permute-done((bf16[360,256]{1,0:T(8,128)(2,1)S(1)}, bf16[360,256]{1,0:T(8,128)(2,1)S(1)}, u32[]{:S(2)}, u32[]{:S(2)}) %collective-permute-start.1) | collective-permute-done | bytes 184352 | tf_op jit(solution)/shard_map/ppermute | solution.py:39
  75.0 0.1 pad_maximum_fusion.refs_1_
  75.1 1.4 collective-permute-start.4
  76.6 0.0 all-to-all-done.1
  76.6 10.8 %all-to-all-start = ((bf16[64,96,128]{2,1,0:T(8,128)(2,1)}), bf16[64,96,128]{2,1,0:T(8,128)(2,1)}, u32[]{:S(2)}, u32[]{:S(2)}) async-start(bf16[64,96,128]{2,1,0:T(8,128)(2,1)} %relayout_last.1), calls=%async_computation | async-start | bytes 3145728 | tf_op jit(solution)/shard_map/all_to_all | solution.py:35
  87.4 1.2 slice.4
  88.6 0.0 copy-start.1
  88.6 0.6 collective-permute-start
  89.2 7.1 %bases.1 = (bf16[768,1536]{1,0:T(8,128)(2,1)}, bf16[1536,768]{1,0:T(8,128)(2,1)}, bf16[512,512]{1,0:T(8,128)(2,1)}, bf16[512,512]{1,0:T(8,128)(2,1)}) custom-call(), custom_call_target="tpu_custom_call" | custom-call | flops 12000000000 | bytes 1048576 | tf_op jit(solution)/shard_map/bases/pallas_call | solution.py:284
  96.3 0.0 collective-permute-done.4.refs_2_
  96.3 0.0 copy-done.1
  96.3 0.8 arrange.1.refs_4_
  97.1 0.0 copy-start.3
  97.1 1.1 copy-done.3
  98.2 0.0 collective-permute-done
  98.2 0.0 copy-start.4
  98.2 0.9 copy-done.4
  99.1 15.4 %member_pair.1.refs_9_ = bf16[4,16,96,128]{3,2,1,0:T(8,128)(2,1)} custom-call(s32[4]{0:T(128)} %pad_add_fusion.refs_0_, bf16[4,16,240,128]{3,2,1,0:T(8,128)(2,1)} %bitcast.7.refs_1_.refs_2_, bf16[4,16,240,128]{3,2,1,0:T(8,128)(2,1)} %bitcast.7.refs_1_.refs_2_, bf16[4,16,48,128]{3,2,1,0:T(8,128)(2,1)} %bitcast.22, bf16[4,1472,128]{2,1,0:T(8,128)(2,1)} %copy-done.3, ...), custom_call_target="tpu_custom_call" | custom-call | flops 12000000000 | bytes 1048576 | tf_op jit(solution)/shard_map/member_pair/pallas_call | solution.py:513
  114.4 0.0 all-to-all-done
  114.5 9.9 %member_last.1 = (bf16[4,16,48,128]{3,2,1,0:T(8,128)(2,1)}, bf16[4,16,48,128]{3,2,1,0:T(8,128)(2,1)}) custom-call(s32[4]{0:T(128)} %pad_add_fusion.refs_0_, bf16[4,16,96,128]{3,2,1,0:T(8,128)(2,1)} %bitcast.5.refs_1_, bf16[4,16,240,128]{3,2,1,0:T(8,128)(2,1)} %bitcast.7.refs_1_.refs_2_, bf16[4,16,48,128]{3,2,1,0:T(8,128)(2,1)} %bitcast.23, ...), custom_call_target="tpu_custom_call" | custom-call | flops 6000000000 | bytes 1048576 | tf_op jit(solution)/shard_map/member_last/pallas_call | solution.py:513
  124.4 0.3 collective-permute-start.5
  124.6 2.3 %collective-permute-done.5 = bf16[4,16,48,128]{3,2,1,0:T(8,128)(2,1)S(1)} collective-permute-done((bf16[4,16,48,128]{3,2,1,0:T(8,128)(2,1)}, bf16[4,16,48,128]{3,2,1,0:T(8,128)(2,1)S(1)}, u32[]{:S(2)}, u32[]{:S(2)}) %collective-permute-start.5) | collective-permute-done | bytes 786464 | tf_op jit(solution)/shard_map/ppermute | solution.py:43
  126.9 0.0 copy-start.2
  126.9 1.3 add_convert_fusion
  128.3 25.3 %all_to_all.15.refs_1_ = bf16[64,48,128]{2,1,0:T(8,128)(2,1)S(1)} all-to-all(bf16[64,48,128]{2,1,0:T(8,128)(2,1)S(1)} %bitcast.18), channel_id=1, replica_groups=mesh['lat'=4,'lon'=16,'mem'=2] {'lat','lon'}, dimensions={0} | all-to-all | bytes 1572864 | tf_op jit(solution)/shard_map/all_to_all | solution.py:35
  153.6 1.6 collective-permute-start.6
  155.2 1.9 %collective-permute-done.6.refs_2_ = bf16[64,48,128]{2,1,0:T(8,128)(2,1)S(1)} collective-permute-done((bf16[64,48,128]{2,1,0:T(8,128)(2,1)S(1)}, bf16[64,48,128]{2,1,0:T(8,128)(2,1)S(1)}, u32[]{:S(2)}, u32[]{:S(2)}) %collective-permute-start.6) | collective-permute-done | bytes 786464 | tf_op jit(solution)/shard_map/ppermute | solution.py:43
  157.1 0.0 copy-done.2
  157.1 2.1 %finish.1 = f32[90,16,128]{2,1,0:T(8,128)} custom-call(s32[4]{0:T(128)S(1)} %copy-done.2, bf16[64,48,128]{2,1,0:T(8,128)(2,1)S(1)} %all_to_all.15.refs_1_, bf16[64,48,128]{2,1,0:T(8,128)(2,1)S(1)} %collective-permute-done.6.refs_2_), custom_call_target="tpu_custom_call" | custom-call | tf_op jit(solution)/shard_map/finish/pallas_call | solution.py:548
  (2 shorter events, 0.1 us)
Async XLA Ops:
  0.0 22.3 %copy-start = (f32[1,360,512]{2,1,0:T(8,128)S(1)}, f32[1,360,512]{2,1,0:T(8,128)}, u32[]{:S(2)}) copy-start(f32[1,360,512]{2,1,0:T(8,128)} %param.7) | copy-start | bytes 2211844
  10.0 66.5 %all-to-all-start.1 = ((bf16[64,240,128]{2,1,0:T(8,128)(2,1)}), bf16[64,240,128]{2,1,0:T(8,128)(2,1)}, u32[]{:S(2)}, u32[]{:S(2)}) async-start(bf16[64,240,128]{2,1,0:T(8,128)(2,1)} %head.1), calls=%async_computation.1 | async-start | bytes 7864320 | tf_op jit(solution)/shard_map/all_to_all | solution.py:35
  22.3 47.3 %collective-permute-start.3 = (bf16[360,256]{1,0:T(8,128)(2,1)S(1)}, bf16[360,256]{1,0:T(8,128)(2,1)S(1)}, u32[]{:S(2)}, u32[]{:S(2)}) collective-permute-start(bf16[360,256]{1,0:T(8,128)(2,1)S(1)} %fusion), channel_id=1, source_target_pairs={{0,96},{32,0},{64,32},{96,64},{1,97},{33,1},{65,33},{97,65},{2,98}... | collective-permute-start | bytes 552968 | tf_op jit(solution)/shard_map/ppermute | solution.py:39
  24.7 47.1 %collective-permute-start.2 = (bf16[360,256]{1,0:T(8,128)(2,1)S(1)}, bf16[360,256]{1,0:T(8,128)(2,1)S(1)}, u32[]{:S(2)}, u32[]{:S(2)}) collective-permute-start(bf16[360,256]{1,0:T(8,128)(2,1)S(1)} %fusion), channel_id=1, source_target_pairs={{0,64},{32,96},{64,0},{96,32},{1,65},{33,97},{65,1},{97,33},{2,66}... | collective-permute-start | bytes 552968 | tf_op jit(solution)/shard_map/ppermute | solution.py:39
  25.1 49.9 %collective-permute-start.1 = (bf16[360,256]{1,0:T(8,128)(2,1)S(1)}, bf16[360,256]{1,0:T(8,128)(2,1)S(1)}, u32[]{:S(2)}, u32[]{:S(2)}) collective-permute-start(bf16[360,256]{1,0:T(8,128)(2,1)S(1)} %fusion), channel_id=1, source_target_pairs={{0,32},{32,64},{64,96},{96,0},{1,33},{33,65},{65,97},{97,1},{2,34}... | collective-permute-start | bytes 552968 | tf_op jit(solution)/shard_map/ppermute | solution.py:39
  75.1 21.1 %collective-permute-start.4 = (bf16[4,360,256]{2,1,0:T(8,128)(2,1)S(1)}, bf16[4,360,256]{2,1,0:T(8,128)(2,1)S(1)}, u32[]{:S(2)}, u32[]{:S(2)}) collective-permute-start(bf16[4,360,256]{2,1,0:T(8,128)(2,1)S(1)} %pad_maximum_fusion.refs_1_), channel_id=1, source_target_pairs={{0,1},{1,0},{2,3},{3,2},{4,5},{5,4},{6,7},{7,6},{8,9},{9,8},{10,11... | collective-permute-start | bytes 2211848 | tf_op jit(solution)/shard_map/ppermute | solution.py:43
  76.6 37.9 %all-to-all-start = ((bf16[64,96,128]{2,1,0:T(8,128)(2,1)}), bf16[64,96,128]{2,1,0:T(8,128)(2,1)}, u32[]{:S(2)}, u32[]{:S(2)}) async-start(bf16[64,96,128]{2,1,0:T(8,128)(2,1)} %relayout_last.1), calls=%async_computation | async-start | bytes 3145728 | tf_op jit(solution)/shard_map/all_to_all | solution.py:35
  88.6 7.6 %copy-start.1 = (s32[4]{0:T(128)S(1)}, s32[4]{0:T(128)}, u32[]{:S(2)}) copy-start(s32[4]{0:T(128)} %pad_add_fusion.refs_0_) | copy-start | bytes 52
  88.6 9.6 %collective-permute-start = (bf16[64,48,128]{2,1,0:T(8,128)(2,1)S(1)}, bf16[64,48,128]{2,1,0:T(8,128)(2,1)S(1)}, u32[]{:S(2)}, u32[]{:S(2)}) collective-permute-start(bf16[64,48,128]{2,1,0:T(8,128)(2,1)S(1)} %slice.4), channel_id=1, source_target_pairs={{0,1},{1,0},{2,3},{3,2},{4,5},{5,4},{6,7},{7,6},{8,9},{9,8},{10,11... | collective-permute-start | bytes 2359304 | tf_op jit(solution)/shard_map/ppermute | solution.py:43
  97.1 1.1 copy-start.3
  98.2 0.9 copy-start.4
  124.4 2.6 %collective-permute-start.5 = (bf16[4,16,48,128]{3,2,1,0:T(8,128)(2,1)}, bf16[4,16,48,128]{3,2,1,0:T(8,128)(2,1)S(1)}, u32[]{:S(2)}, u32[]{:S(2)}) collective-permute-start(bf16[4,16,48,128]{3,2,1,0:T(8,128)(2,1)} %get-tuple-element.16), channel_id=1, source_target_pairs={{0,1},{1,0},{2,3},{3,2},{4,5},{5,4},{6,7},{7,6},{8,9},{9,8},{10,11... | collective-permute-start | bytes 2359304 | tf_op jit(solution)/shard_map/ppermute | solution.py:43
  126.9 30.2 %copy-start.2 = (s32[4]{0:T(128)S(1)}, s32[4]{0:T(128)}, u32[]{:S(2)}) copy-start(s32[4]{0:T(128)} %pad_add_fusion.refs_0_) | copy-start | bytes 52
  153.6 3.5 %collective-permute-start.6 = (bf16[64,48,128]{2,1,0:T(8,128)(2,1)S(1)}, bf16[64,48,128]{2,1,0:T(8,128)(2,1)S(1)}, u32[]{:S(2)}, u32[]{:S(2)}) collective-permute-start(bf16[64,48,128]{2,1,0:T(8,128)(2,1)S(1)} %all_to_all.15.refs_1_), channel_id=1, source_target_pairs={{0,1},{1,0},{2,3},{3,2},{4,5},{5,4},{6,7},{7,6},{8,9},{9,8},{10,11... | collective-permute-start | bytes 2359304 | tf_op jit(solution)/shard_map/ppermute | solution.py:43

commit v3 on v2

--- a/solution.py
+++ b/solution.py
@@ -95,30 +95,45 @@
             fields_in[p, g, LEAD + cols + 1 :] = jnp.zeros((LEAD - 1, levels, 128), BF)
     slots = levels * half
     acc[...] = jnp.zeros_like(acc)
-    slot_ids = lax.broadcasted_iota(jnp.int32, (slots, 128), 0)
-    row_ids = lax.broadcasted_iota(jnp.int32, (128, 128), 0)
+
+    def spots_of(count):
+        major = lax.broadcasted_iota(jnp.int32, (count // 16, 16, 128), 0)
+        minor = lax.broadcasted_iota(jnp.int32, (count // 16, 16, 128), 1)
+        return (major * 16 + minor).astype(F32).astype(BF)
+
+    def packed(row):
+        return jnp.broadcast_to(row, (16, 128)).astype(BF)[None]
+
+    slot_ids = spots_of(256)
+    row_ids = spots_of(128)
+    one = jnp.ones((), BF)
+    zero = jnp.zeros((), BF)
     for copy in observed:
         copy.wait()
 
     def add_group(g, carry):
-        rows = pl.ds(pl.multiple_of(g * 8, 8), 8)
+        rows = pl.ds(pl.multiple_of(g * 16, 8), 16)
         column = col_ref[rows, :] - lon * cols
         within = jnp.where(mirrored & (column > 0), cols - column, column) - mem * half
         inside = (within >= 0) & (within < half)
         keys = jnp.where(inside, level_ref[rows, :] * half + within, -1)
-        lat_row = row_ref[rows, :] - lat * 128
+        lat_row = (row_ref[rows, :] - lat * 128).astype(F32)
         value = value_ref[rows, :]
         high = value.astype(BF).astype(F32)
         middle = value - high
+        parts = []
+        for start in range(0, slots, 256):
+            part = keys - start
+            parts.append(jnp.where((part >= 0) & (part < 256), part, -1).astype(F32))
         left = []
         right = []
-        for r in range(8):
-            hit = slot_ids == keys[r : r + 1, :]
-            left.append(jnp.where(hit, 1.0, 0.0).astype(BF))
-            row_hit = row_ids == lat_row[r : r + 1, :]
-            top = jnp.where(row_hit, high[r : r + 1, :], 0.0)
-            low = jnp.where(row_hit, middle[r : r + 1, :], 0.0)
-            right.append(jnp.concatenate([top, low], axis=0).astype(BF))
+        for r in range(16):
+            at = slice(r, r + 1)
+            hits = [jnp.where(slot_ids == packed(part[at]), one, zero).reshape(256, 128) for part in parts]
+            left.append(jnp.concatenate(hits, axis=0))
+            row_hit = row_ids == packed(lat_row[at])
+            sides = [jnp.where(row_hit, packed(side[at]), zero).reshape(128, 128) for side in (high, middle)]
+            right.append(jnp.concatenate(sides, axis=0))
         acc[...] += lax.dot_general(
             jnp.concatenate(left, axis=1),
             jnp.concatenate(right, axis=1),
@@ -127,30 +142,37 @@
         )
         return carry
 
-    lax.fori_loop(0, row_ref.shape[0] // 8, add_group, 0)
-    innov[...] = (acc[:, :128] + acc[:, 128:]).astype(BF).reshape(levels, half, 128)
-    leaving = [
-        fetch(innov, out.at[pl.ds(g * levels, levels), pl.ds(2 * padded, half), :]) for g in range(bands)
-    ]
+    leaving = []
+    lax.fori_loop(0, 2, add_group, 0)
     turn = turner(levels, mirrored, 16)
     last_turn = turner(levels, mirrored, cols % 16)
-    for g in range(bands):
-        for copy in arriving[g]:
-            copy.wait()
+    for first in range(0, bands, 2):
+        group = range(first, first + 2)
+        for g in group:
+            for copy in arriving[g]:
+                copy.wait()
         for start in range(0, padded, 16):
             rows = pl.ds(turn_start(start, mirrored, cols), 16)
             matrix = turn if start + 16 <= cols else last_turn
-            turned = turn_block([fields_in[p, g, rows] for p in range(2)], matrix, levels)
+            turned = turn_block([fields_in[p, g, rows] for g in group for p in range(2)], matrix, levels)
             for l in range(levels):
-                for p in range(2):
-                    piece = turned[16 * l : 16 * l + 16, 128 * p : 128 * p + 128]
-                    staged[g * levels + l, p * padded + start : p * padded + start + 16, :] = piece
-        leaving.append(
-            fetch(
-                staged.at[pl.ds(g * levels, levels)],
-                out.at[pl.ds(g * levels, levels), pl.ds(0, 2 * padded), :],
+                for n, g in enumerate(group):
+                    for p in range(2):
+                        lane = 256 * n + 128 * p
+                        piece = turned[16 * l : 16 * l + 16, lane : lane + 128]
+                        staged[g * levels + l, p * padded + start : p * padded + start + 16, :] = piece
+        for g in group:
+            leaving.append(
+                fetch(
+                    staged.at[pl.ds(g * levels, levels)],
+                    out.at[pl.ds(g * levels, levels), pl.ds(0, 2 * padded), :],
+                )
             )
-        )
+    lax.fori_loop(2, row_ref.shape[0] // 16, add_group, 0)
+    innov[...] = (acc[:, :128] + acc[:, 128:]).astype(BF).reshape(levels, half, 128)
+    leaving += [
+        fetch(innov, out.at[pl.ds(g * levels, levels), pl.ds(2 * padded, half), :]) for g in range(bands)
+    ]
     for copy in leaving:
         copy.wait()
 
@@ -321,12 +343,13 @@
 
 
 def member_kernel(*refs, first, final, count, blocks, bands, padded, coefs):
-    place, field_hbm, pair_hbm, other_hbm, taper_hbm, lon_hbm, lon_t_hbm, lat_hbm, lat_t_hbm = refs[:9]
+    place, field_in, own_in, other_in, taper_hbm, lon_hbm, lon_t_hbm, lat_hbm, lat_t_hbm = refs[:9]
     rest = list(refs[9:])
     so_far_hbm = None if first else rest.pop(0)
     outs = [rest.pop(0) for _ in range(2 if final else 1)]
-    folded, inverse, field, innov, taper, lon_ref, lon_t_ref, lat_ref, lat_t_ref, acc, sems = rest[:11]
-    stages = rest[11:]
+    folded, inverse, taper, lon_ref, lon_t_ref, lat_ref, lat_t_ref, acc, sems = rest[:9]
+    stages = rest[9 : 9 + len(outs)]
+    field, own, other = (field_in, own_in, other_in) if final else rest[9 + len(outs) :]
     pairs = blocks // 2
     tall = padded * pairs
     nyquist = coefs // 2
@@ -336,8 +359,6 @@
     turns = pairs // group
     half = padded // 2
     mem = place[0]
-    own_rows = pl.ds(pl.multiple_of(mem * half, half), half)
-    other_rows = pl.ds(pl.multiple_of((1 - mem) * half, half), half)
 
     def move(source, target, spot):
         return pltpu.make_async_copy(source, target, sems.at[spot])
@@ -361,13 +382,13 @@
         at = spots(b, side)
         return move(stages[n].at[:, at], outs[n].at[:, at], 22 + 4 * n + 2 * b + side)
 
-    innov_copies = [
-        move(pair_hbm.at[:, :, pl.ds(2 * padded, half), :], innov.at[:, :, own_rows, :], 0),
-        move(other_hbm, innov.at[:, :, other_rows, :], 1),
-    ]
-    field_copies = [
-        move(field_hbm.at[a, :, pl.ds(0, count * padded), :], field.at[a], 2 + a) for a in range(bands)
-    ]
+    field_copies = []
+    if not final:
+        field_copies = [
+            move(own_in, own, 0),
+            move(other_in, other, 1),
+            *[move(field_in.at[a, :, pl.ds(0, count * padded), :], field.at[a], 2 + a) for a in range(bands)],
+        ]
     table_copies = [
         lon_t_copy(0),
         lon_t_copy(2),
@@ -375,18 +396,22 @@
         move(taper_hbm, taper, 8),
         move(lat_t_hbm, lat_t_ref, 9),
     ]
-    for copy in innov_copies + field_copies + table_copies:
+    for copy in field_copies + table_copies:
         copy.start()
     for side in range(2):
         inverse[side, 2 * step :, :] = jnp.zeros((tall - 2 * step, inverse.shape[2]), BF)
-    for copy in innov_copies:
+    for copy in field_copies:
         copy.wait()
     down = lax.broadcasted_iota(jnp.int32, (padded, 128), 0)
     cols = coefs // blocks
 
     def weigh(i, a):
         def product(j):
-            return field[a, j, i * padded : (i + 1) * padded, :].astype(F32) * innov[a, j].astype(F32)
+            mine, theirs = own[a, j], other[a, j]
+            innov = jnp.concatenate(
+                [jnp.where(mem == 0, mine, theirs), jnp.where(mem == 0, theirs, mine)], axis=0
+            )
+            return field[a, j, i * padded : (i + 1) * padded, :].astype(F32) * innov.astype(F32)
 
         def body(j, carry):
             rows = pl.ds(pl.multiple_of(j * padded, padded), padded)
@@ -415,6 +440,13 @@
                 jnp.dot(lon_t_ref[tables[side], :], folded[side], preferred_element_type=F32).astype(BF)
                 for side in range(2)
             ]
+            if fresh:
+
+                @pl.when(r == 0)
+                def _():
+                    for copy in table_copies[2:]:
+                        copy.wait()
+
             spectrum = [jnp.dot(zonal[side], lat_ref[...], preferred_element_type=F32) for side in range(2)]
             tapered = []
             for side in range(2):
@@ -479,14 +511,13 @@
             body(b, 0)
 
     for i in range(count):
-        for a in range(bands):
-            if i == 0:
-                field_copies[a].wait()
-            weigh(i, a)
         if i == 0:
             for r in (1, 3):
                 lon_t_copy(r).start()
-            for copy in table_copies:
+        for a in range(bands):
+            weigh(i, a)
+        if i == 0:
+            for copy in table_copies[:2]:
                 copy.wait()
         spectral(i == 0)
         gridded(i)
@@ -496,16 +527,18 @@
             out_copy(b, 1, n).wait()
 
 
-def member(place, field, pair, other, taper, tables, so_far, final, dims):
+def member(place, field, own, other, taper, tables, so_far, final, dims):
     _, blocks, bands, padded, coefs, lat_total = dims
     half = padded // 2
     tall = padded * blocks // 2
     first = so_far is None
     count = 1 if final else 2
     split = lambda array: array.reshape(bands, blocks, *array.shape[1:])
-    far = [split(field), split(pair), split(other), taper, *tables] + ([] if first else [so_far])
+    near = [split(field), split(own), split(other)]
+    far = [taper, *tables] + ([] if first else [so_far])
     block = lambda rows, dtype: ((bands, blocks, rows, 128), dtype)
-    scratch = [((2, tall, lat_total), BF), ((2, tall, lat_total), BF), block(count * padded, BF), block(padded, BF)]
+    scratch = [((2, tall, lat_total), BF), ((2, tall, lat_total), BF)]
+    fields = [] if final else [block(count * padded, BF), block(half, BF), block(half, BF)]
     scratch += [(array.shape, array.dtype) for array in (taper, *tables)]
     scratch.append(block(padded, F32 if first else BF))
     results = [block(half, BF), block(half, BF)] if final else [block(padded, BF)]
@@ -515,15 +548,15 @@
             *refs, first=first, final=final, count=count, blocks=blocks, bands=bands, padded=padded, coefs=coefs
         ),
         out_shape=[jax.ShapeDtypeStruct(*each) for each in results],
-        in_specs=[sspec()] + [hbm] * len(far),
+        in_specs=[sspec()] + [vspec() if final else hbm] * len(near) + [hbm] * len(far),
         out_specs=[hbm] * len(results),
         scratch_shapes=[pltpu.VMEM(*each) for each in scratch]
         + [pltpu.SemaphoreType.DMA((32,))]
-        + [pltpu.VMEM(*each) for each in results],
-        compiler_params=params(60),
+        + [pltpu.VMEM(*each) for each in results + fields],
+        compiler_params=params(62),
         cost_estimate=cost(count * 6e9),
         name="member_last" if final else "member_pair",
-    )(place, *far)
+    )(place, *near, *far)
 
 
 def finish_kernel(place, own, other, out, *, levels, cols, half, scale):
@@ -577,14 +610,15 @@
         ring.append(shift_lat(taper_mine, u))
     last_out = relayout_last(place, by_round, padded)
     last = over_all(last_out)
-    own = jnp.stack(ring)
-    weights = arrange(place, own, swap(own))
-    other = swap(pair[:, 2 * padded :, :])
+    stacked = jnp.stack(ring)
+    weights = arrange(place, stacked, swap(stacked))
+    own = pair[:, 2 * padded :, :]
+    other = swap(own)
 
     tables = bases(cols, blocks, padded, lat_total)
     dims = (cols, blocks, bands, padded, coefs, lat_total)
-    (summed,) = member(place, pair, pair, other, weights, tables, None, False, dims)
-    mine, theirs = member(place, last, pair, other, weights, tables, summed, True, dims)
+    (summed,) = member(place, pair, own, other, weights, tables, None, False, dims)
+    mine, theirs = member(place, last, own, other, weights, tables, summed, True, dims)
     merged = (mine.astype(F32) + swap(theirs).astype(F32)).astype(BF).reshape(bands * blocks, half, lat_rows)
     pieces = over_all(merged)
     out = finish(place, pieces, swap(pieces), levels, cols, half, 1.0 / (ensemble - 1))

time: 160 us -> 158 us (0.988)
  waiting for transfers between devices: 50.5 us -> 48.9 us
  transfers between devices with their start and end apart: 9 -> 9, of which waited for: 5 -> 4; matrix products, arithmetic and copies ran while one was open for 1% -> 1% of each run, Pallas kernels for 16% -> 17%
where the time goes in v3:
time: 158 us; the launch traced here: 157 us
  waiting for transfers between devices  48.9 us (31%)
  Pallas kernels  46.3 us (29%)
  starting transfers between devices  31.3 us (20%)
  blocking collectives  25.3 us (16%)
  local copies, waits for them, and re-layouts  3.32 us (2%)
  other arithmetic  2.05 us (1%)
    ppermute x3, waiting for transfers between devices, shift_lat(): return lax.ppermute(x, 'lat', [(i, (i + s) % RING) for i in range(RING)])  44.7 us
    all_to_all x1, blocking collectives, over_all(): return lax.all_to_all(x, LL, split_axis=0, concat_axis=0, tiled=True)  25.3 us
    pallas_call x2, Pallas kernels, member(): pl.pallas_call(lambda *refs: member_kernel(*refs, first=first, final=fina...  25.3 us
    all_to_all x2, starting transfers between devices, over_all(): return lax.all_to_all(x, LL, split_axis=0, concat_axis=0, tiled=True)  22.4 us
    pallas_call x1, Pallas kernels, head(): pl.pallas_call(lambda *refs: head_kernel(*refs, half=half, levels=levels,...  8.02 us
    pallas_call x1, Pallas kernels, bases(): pl.pallas_call(lambda *refs: basis_kernel(*refs, cols=cols, blocks=blocks...  7.02 us
    ppermute x3, starting transfers between devices, shift_lat(): return lax.ppermute(x, 'lat', [(i, (i + s) % RING) for i in range(RING)])  4.69 us
    ppermute x4, waiting for transfers between devices, swap(): return lax.ppermute(x, 'mem', SWAP)  4.22 us
  transfers between devices with their start and end apart: 9, of which 4 were waited for; matrix products, arithmetic and copies ran while one was open for 1% of the time, Pallas kernels for 17%

profile of v3, /device:TPU:1, one launch (start us, length us, event | category | flops | bytes accessed | tf_op | source)
XLA Modules:
  0.0 157.4 jit_solution(6103072388341449264)
XLA Ops:
  0.0 0.0 copy-start
  0.0 0.6 pad_add_fusion.refs_0_
  0.6 8.0 %head.1 = bf16[64,240,128]{2,1,0:T(8,128)(2,1)} custom-call(s32[4]{0:T(128)} %pad_add_fusion.refs_0_, bf16[3,4,90,16,128]{4,3,2,1,0:T(8,128)(2,1)} %bitcast.17, s32[64,128]{1,0:T(8,128)} %refs_2_.1, s32[64,128]{1,0:T(8,128)} %refs_3_.1, s32[64,128]{1,0:T(8,128)} %refs_4_.1, f32[64,128]{1,0:T(8,128)} %refs_5_.1), custom_call_target="tpu_custom_call" | custom-call | flops 6000000000 | bytes 1048576 | tf_op jit(solution)/shard_map/head/pallas_call | solution.py:185
  8.6 12.2 %all-to-all-start.1 = ((bf16[64,240,128]{2,1,0:T(8,128)(2,1)}), bf16[64,240,128]{2,1,0:T(8,128)(2,1)}, u32[]{:S(2)}, u32[]{:S(2)}) async-start(bf16[64,240,128]{2,1,0:T(8,128)(2,1)} %head.1), calls=%async_computation.1 | async-start | bytes 7864320 | tf_op jit(solution)/shard_map/all_to_all | solution.py:35
  20.8 0.0 copy-done
  20.9 1.0 collective-permute-start.1
  21.9 2.6 %collective-permute-start.2 = (bf16[360,256]{1,0:T(8,128)(2,1)S(1)}, bf16[360,256]{1,0:T(8,128)(2,1)S(1)}, u32[]{:S(2)}, u32[]{:S(2)}) collective-permute-start(bf16[360,256]{1,0:T(8,128)(2,1)S(1)} %fusion), channel_id=1, source_target_pairs={{0,64},{32,96},{64,0},{96,32},{1,65},{33,97},{65,1},{97,33},{2,66}... | collective-permute-start | bytes 552968 | tf_op jit(solution)/shard_map/ppermute | solution.py:39
  24.5 1.1 collective-permute-start.3
  25.6 3.0 %relayout_last.1 = bf16[64,96,128]{2,1,0:T(8,128)(2,1)} custom-call(s32[4]{0:T(128)} %pad_add_fusion.refs_0_, bf16[3,4,90,16,128]{4,3,2,1,0:T(8,128)(2,1)} %bitcast.18), custom_call_target="tpu_custom_call" | custom-call | tf_op jit(solution)/shard_map/relayout_last/pallas_call | solution.py:225
  28.6 40.4 %collective-permute-done.1 = bf16[360,256]{1,0:T(8,128)(2,1)S(1)} collective-permute-done((bf16[360,256]{1,0:T(8,128)(2,1)S(1)}, bf16[360,256]{1,0:T(8,128)(2,1)S(1)}, u32[]{:S(2)}, u32[]{:S(2)}) %collective-permute-start.1) | collective-permute-done | bytes 184352 | tf_op jit(solution)/shard_map/ppermute | solution.py:39
  69.0 4.3 %collective-permute-done.2 = bf16[360,256]{1,0:T(8,128)(2,1)S(1)} collective-permute-done((bf16[360,256]{1,0:T(8,128)(2,1)S(1)}, bf16[360,256]{1,0:T(8,128)(2,1)S(1)}, u32[]{:S(2)}, u32[]{:S(2)}) %collective-permute-start.2) | collective-permute-done | bytes 184352 | tf_op jit(solution)/shard_map/ppermute | solution.py:39
  73.3 0.0 collective-permute-done.3
  73.3 0.1 pad_maximum_fusion.refs_1_
  73.4 1.8 %collective-permute-start.4 = (bf16[4,360,256]{2,1,0:T(8,128)(2,1)S(1)}, bf16[4,360,256]{2,1,0:T(8,128)(2,1)S(1)}, u32[]{:S(2)}, u32[]{:S(2)}) collective-permute-start(bf16[4,360,256]{2,1,0:T(8,128)(2,1)S(1)} %pad_maximum_fusion.refs_1_), channel_id=1, source_target_pairs={{0,1},{1,0},{2,3},{3,2},{4,5},{5,4},{6,7},{7,6},{8,9},{9,8},{10,11... | collective-permute-start | bytes 2211848 | tf_op jit(solution)/shard_map/ppermute | solution.py:43
  75.2 0.0 all-to-all-done.1
  75.2 10.2 %all-to-all-start = ((bf16[64,96,128]{2,1,0:T(8,128)(2,1)}), bf16[64,96,128]{2,1,0:T(8,128)(2,1)}, u32[]{:S(2)}, u32[]{:S(2)}) async-start(bf16[64,96,128]{2,1,0:T(8,128)(2,1)} %relayout_last.1), calls=%async_computation | async-start | bytes 3145728 | tf_op jit(solution)/shard_map/all_to_all | solution.py:35
  85.4 1.2 slice.4
  86.6 0.0 copy-start.4
  86.6 0.0 copy-start.1
  86.6 0.6 collective-permute-start
  87.2 7.0 %bases.1 = (bf16[768,1536]{1,0:T(8,128)(2,1)}, bf16[1536,768]{1,0:T(8,128)(2,1)}, bf16[512,512]{1,0:T(8,128)(2,1)}, bf16[512,512]{1,0:T(8,128)(2,1)}) custom-call(), custom_call_target="tpu_custom_call" | custom-call | flops 12000000000 | bytes 1048576 | tf_op jit(solution)/shard_map/bases/pallas_call | solution.py:306
  94.2 0.0 copy-done.4
  94.2 0.0 collective-permute-done.4.refs_2_
  94.2 0.0 copy-done.1
  94.2 0.8 arrange.1.refs_4_
  95.0 0.0 copy-start.3
  95.0 1.1 copy-done.3
  96.2 0.0 collective-permute-done
  96.2 0.0 copy-start.5
  96.2 0.9 copy-done.5
  97.1 15.6 %member_pair.1.refs_9_ = bf16[4,16,96,128]{3,2,1,0:T(8,128)(2,1)} custom-call(s32[4]{0:T(128)} %pad_add_fusion.refs_0_, bf16[4,16,240,128]{3,2,1,0:T(8,128)(2,1)} %bitcast.13.refs_1_, bf16[4,16,48,128]{3,2,1,0:T(8,128)(2,1)} %bitcast.20, bf16[4,16,48,128]{3,2,1,0:T(8,128)(2,1)} %bitcast.25, bf16[4,1472,128]{2,1,0:T(8,128)(2,1)} %copy-done.3, ...), custom_call_target="tpu_custom_call" | custom-call | flops 12000000000 | bytes 1048576 | tf_op jit(solution)/shard_map/member_pair/pallas_call | solution.py:546
  112.7 0.0 all-to-all-done
  112.7 9.7 %member_last.1 = (bf16[4,16,48,128]{3,2,1,0:T(8,128)(2,1)}, bf16[4,16,48,128]{3,2,1,0:T(8,128)(2,1)}) custom-call(s32[4]{0:T(128)} %pad_add_fusion.refs_0_, bf16[4,16,96,128]{3,2,1,0:T(8,128)(2,1)} %bitcast.5.refs_1_, bf16[4,16,48,128]{3,2,1,0:T(8,128)(2,1)} %bitcast.21, bf16[4,16,48,128]{3,2,1,0:T(8,128)(2,1)} %bitcast.26, bf16[4,1472,128]{2,1,0:T(8,128)(2,1)} %copy-done.3, ...), custom_call_target="tpu_custom_call" | custom-call | flops 6000000000 | bytes 1048576 | tf_op jit(solution)/shard_map/member_last/pallas_call | solution.py:546
  122.5 0.3 collective-permute-start.5
  122.7 2.3 %collective-permute-done.5 = bf16[4,16,48,128]{3,2,1,0:T(8,128)(2,1)S(1)} collective-permute-done((bf16[4,16,48,128]{3,2,1,0:T(8,128)(2,1)}, bf16[4,16,48,128]{3,2,1,0:T(8,128)(2,1)S(1)}, u32[]{:S(2)}, u32[]{:S(2)}) %collective-permute-start.5) | collective-permute-done | bytes 786464 | tf_op jit(solution)/shard_map/ppermute | solution.py:43
  125.0 0.0 copy-start.2
  125.0 1.3 add_convert_fusion
  126.4 25.3 %all_to_all.15.refs_1_ = bf16[64,48,128]{2,1,0:T(8,128)(2,1)S(1)} all-to-all(bf16[64,48,128]{2,1,0:T(8,128)(2,1)S(1)} %bitcast.19), channel_id=1, replica_groups=mesh['lat'=4,'lon'=16,'mem'=2] {'lat','lon'}, dimensions={0} | all-to-all | bytes 1572864 | tf_op jit(solution)/shard_map/all_to_all | solution.py:35
  151.7 1.6 %collective-permute-start.6 = (bf16[64,48,128]{2,1,0:T(8,128)(2,1)S(1)}, bf16[64,48,128]{2,1,0:T(8,128)(2,1)S(1)}, u32[]{:S(2)}, u32[]{:S(2)}) collective-permute-start(bf16[64,48,128]{2,1,0:T(8,128)(2,1)S(1)} %all_to_all.15.refs_1_), channel_id=1, source_target_pairs={{0,1},{1,0},{2,3},{3,2},{4,5},{5,4},{6,7},{7,6},{8,9},{9,8},{10,11... | collective-permute-start | bytes 2359304 | tf_op jit(solution)/shard_map/ppermute | solution.py:43
  153.3 1.9 %collective-permute-done.6.refs_2_ = bf16[64,48,128]{2,1,0:T(8,128)(2,1)S(1)} collective-permute-done((bf16[64,48,128]{2,1,0:T(8,128)(2,1)S(1)}, bf16[64,48,128]{2,1,0:T(8,128)(2,1)S(1)}, u32[]{:S(2)}, u32[]{:S(2)}) %collective-permute-start.6) | collective-permute-done | bytes 786464 | tf_op jit(solution)/shard_map/ppermute | solution.py:43
  155.2 0.0 copy-done.2
  155.2 2.1 %finish.1 = f32[90,16,128]{2,1,0:T(8,128)} custom-call(s32[4]{0:T(128)S(1)} %copy-done.2, bf16[64,48,128]{2,1,0:T(8,128)(2,1)S(1)} %all_to_all.15.refs_1_, bf16[64,48,128]{2,1,0:T(8,128)(2,1)S(1)} %collective-permute-done.6.refs_2_), custom_call_target="tpu_custom_call" | custom-call | tf_op jit(solution)/shard_map/finish/pallas_call | solution.py:581
  (2 shorter events, 0.1 us)
Async XLA Ops:
  0.0 20.8 %copy-start = (f32[1,360,512]{2,1,0:T(8,128)S(1)}, f32[1,360,512]{2,1,0:T(8,128)}, u32[]{:S(2)}) copy-start(f32[1,360,512]{2,1,0:T(8,128)} %param.7) | copy-start | bytes 2211844
  8.6 66.6 %all-to-all-start.1 = ((bf16[64,240,128]{2,1,0:T(8,128)(2,1)}), bf16[64,240,128]{2,1,0:T(8,128)(2,1)}, u32[]{:S(2)}, u32[]{:S(2)}) async-start(bf16[64,240,128]{2,1,0:T(8,128)(2,1)} %head.1), calls=%async_computation.1 | async-start | bytes 7864320 | tf_op jit(solution)/shard_map/all_to_all | solution.py:35
  20.9 48.1 %collective-permute-start.1 = (bf16[360,256]{1,0:T(8,128)(2,1)S(1)}, bf16[360,256]{1,0:T(8,128)(2,1)S(1)}, u32[]{:S(2)}, u32[]{:S(2)}) collective-permute-start(bf16[360,256]{1,0:T(8,128)(2,1)S(1)} %fusion), channel_id=1, source_target_pairs={{0,32},{32,64},{64,96},{96,0},{1,33},{33,65},{65,97},{97,1},{2,34}... | collective-permute-start | bytes 552968 | tf_op jit(solution)/shard_map/ppermute | solution.py:39
  21.9 51.4 %collective-permute-start.2 = (bf16[360,256]{1,0:T(8,128)(2,1)S(1)}, bf16[360,256]{1,0:T(8,128)(2,1)S(1)}, u32[]{:S(2)}, u32[]{:S(2)}) collective-permute-start(bf16[360,256]{1,0:T(8,128)(2,1)S(1)} %fusion), channel_id=1, source_target_pairs={{0,64},{32,96},{64,0},{96,32},{1,65},{33,97},{65,1},{97,33},{2,66}... | collective-permute-start | bytes 552968 | tf_op jit(solution)/shard_map/ppermute | solution.py:39
  24.5 48.8 %collective-permute-start.3 = (bf16[360,256]{1,0:T(8,128)(2,1)S(1)}, bf16[360,256]{1,0:T(8,128)(2,1)S(1)}, u32[]{:S(2)}, u32[]{:S(2)}) collective-permute-start(bf16[360,256]{1,0:T(8,128)(2,1)S(1)} %fusion), channel_id=1, source_target_pairs={{0,96},{32,0},{64,32},{96,64},{1,97},{33,1},{65,33},{97,65},{2,98}... | collective-permute-start | bytes 552968 | tf_op jit(solution)/shard_map/ppermute | solution.py:39
  73.4 20.8 %collective-permute-start.4 = (bf16[4,360,256]{2,1,0:T(8,128)(2,1)S(1)}, bf16[4,360,256]{2,1,0:T(8,128)(2,1)S(1)}, u32[]{:S(2)}, u32[]{:S(2)}) collective-permute-start(bf16[4,360,256]{2,1,0:T(8,128)(2,1)S(1)} %pad_maximum_fusion.refs_1_), channel_id=1, source_target_pairs={{0,1},{1,0},{2,3},{3,2},{4,5},{5,4},{6,7},{7,6},{8,9},{9,8},{10,11... | collective-permute-start | bytes 2211848 | tf_op jit(solution)/shard_map/ppermute | solution.py:43
  75.2 37.5 %all-to-all-start = ((bf16[64,96,128]{2,1,0:T(8,128)(2,1)}), bf16[64,96,128]{2,1,0:T(8,128)(2,1)}, u32[]{:S(2)}, u32[]{:S(2)}) async-start(bf16[64,96,128]{2,1,0:T(8,128)(2,1)} %relayout_last.1), calls=%async_computation | async-start | bytes 3145728 | tf_op jit(solution)/shard_map/all_to_all | solution.py:35
  86.6 7.6 %copy-start.4 = (bf16[64,48,128]{2,1,0:T(8,128)(2,1)}, bf16[64,48,128]{2,1,0:T(8,128)(2,1)S(1)}, u32[]{:S(2)}) copy-start(bf16[64,48,128]{2,1,0:T(8,128)(2,1)S(1)} %slice.4) | copy-start | bytes 2359300
  86.6 7.6 %copy-start.1 = (s32[4]{0:T(128)S(1)}, s32[4]{0:T(128)}, u32[]{:S(2)}) copy-start(s32[4]{0:T(128)} %pad_add_fusion.refs_0_) | copy-start | bytes 52
  86.6 9.6 %collective-permute-start = (bf16[64,48,128]{2,1,0:T(8,128)(2,1)S(1)}, bf16[64,48,128]{2,1,0:T(8,128)(2,1)S(1)}, u32[]{:S(2)}, u32[]{:S(2)}) collective-permute-start(bf16[64,48,128]{2,1,0:T(8,128)(2,1)S(1)} %slice.4), channel_id=1, source_target_pairs={{0,1},{1,0},{2,3},{3,2},{4,5},{5,4},{6,7},{7,6},{8,9},{9,8},{10,11... | collective-permute-start | bytes 2359304 | tf_op jit(solution)/shard_map/ppermute | solution.py:43
  95.0 1.1 copy-start.3
  96.2 0.9 copy-start.5
  122.5 2.6 %collective-permute-start.5 = (bf16[4,16,48,128]{3,2,1,0:T(8,128)(2,1)}, bf16[4,16,48,128]{3,2,1,0:T(8,128)(2,1)S(1)}, u32[]{:S(2)}, u32[]{:S(2)}) collective-permute-start(bf16[4,16,48,128]{3,2,1,0:T(8,128)(2,1)} %get-tuple-element.16), channel_id=1, source_target_pairs={{0,1},{1,0},{2,3},{3,2},{4,5},{5,4},{6,7},{7,6},{8,9},{9,8},{10,11... | collective-permute-start | bytes 2359304 | tf_op jit(solution)/shard_map/ppermute | solution.py:43
  125.0 30.2 %copy-start.2 = (s32[4]{0:T(128)S(1)}, s32[4]{0:T(128)}, u32[]{:S(2)}) copy-start(s32[4]{0:T(128)} %pad_add_fusion.refs_0_) | copy-start | bytes 52
  151.7 3.5 %collective-permute-start.6 = (bf16[64,48,128]{2,1,0:T(8,128)(2,1)S(1)}, bf16[64,48,128]{2,1,0:T(8,128)(2,1)S(1)}, u32[]{:S(2)}, u32[]{:S(2)}) collective-permute-start(bf16[64,48,128]{2,1,0:T(8,128)(2,1)S(1)} %all_to_all.15.refs_1_), channel_id=1, source_target_pairs={{0,1},{1,0},{2,3},{3,2},{4,5},{5,4},{6,7},{7,6},{8,9},{9,8},{10,11... | collective-permute-start | bytes 2359304 | tf_op jit(solution)/shard_map/ppermute | solution.py:43

commit v4 on v3

--- a/solution.py
+++ b/solution.py
@@ -64,7 +64,7 @@
     return jnp.where(mirrored, LEAD + cols - 15 - start, LEAD + start)
 
 
-def head_kernel(place, fields, row_hbm, col_hbm, level_hbm, value_hbm, out, *scratch, half, levels, cols, padded):
+def head_kernel(fields, row_hbm, col_hbm, level_hbm, value_hbm, out, *scratch, half, levels, cols, padded):
     row_ref, col_ref, level_ref, value_ref, fields_in, staged, innov, acc, sems = scratch
     bands = fields.shape[1]
     count = iter(range(32))
@@ -87,8 +87,8 @@
         )
         for g in range(bands)
     ]
-    mem, lat, lon = place[0], place[1], place[2]
-    mirrored = lon >= place[3]
+    mem, lat, lon = lax.axis_index("mem"), lax.axis_index("lat"), lax.axis_index("lon")
+    mirrored = lon >= lax.axis_size("lon") // 2
     for p in range(2):
         for g in range(bands):
             fields_in[p, g, :LEAD] = jnp.zeros((LEAD, levels, 128), BF)
@@ -177,7 +177,7 @@
         copy.wait()
 
 
-def head(place, fields, obs_row, obs_col, obs_level, obs_value, half, padded):
+def head(fields, obs_row, obs_col, obs_level, obs_value, half, padded):
     _, bands, cols, levels, lanes = fields.shape
     rows = 2 * padded + half
     hbm = pl.BlockSpec(memory_space=pltpu.HBM)
@@ -185,7 +185,7 @@
     return pl.pallas_call(
         lambda *refs: head_kernel(*refs, half=half, levels=levels, cols=cols, padded=padded),
         out_shape=jax.ShapeDtypeStruct((bands * levels, rows, lanes), BF),
-        in_specs=[sspec()] + [hbm] * 5,
+        in_specs=[hbm] * 5,
         out_specs=hbm,
         scratch_shapes=[pltpu.VMEM(array.shape, array.dtype) for array in observed]
         + [
@@ -198,7 +198,7 @@
         compiler_params=params(61),
         cost_estimate=cost(6e9),
         name="head",
-    )(place, fields, *observed)
+    )(fields, *observed)
 
 
 def relayout_last_kernel(place, in_ref, out_ref, room, *, cols, levels, padded):
@@ -601,7 +601,8 @@
     place = jnp.stack([mem, lat, lon, jnp.int32(blocks // 2)]).astype(jnp.int32)
 
     by_round = jnp.transpose(anomalies, (0, 2, 1, 3)).reshape(members // bands, bands, cols, levels, lat_rows)
-    pair_out = head(place, by_round, obs_row, obs_col, obs_level, obs_value, half, padded)
+    pair_out = head(by_round, obs_row, obs_col, obs_level, obs_value, half, padded)
+    pair_out, taper = lax.optimization_barrier((pair_out, taper))
     pair = over_all(pair_out)
     n_half = lat_total // 2
     taper_mine = lax.dynamic_slice_in_dim(taper[0], mem * n_half, n_half, axis=1).astype(BF)

time: 158 us -> 157 us (level)
  no operation moved by 1% of the time
where the time goes in v4:
time: 157 us; the launch traced here: 156 us
  waiting for transfers between devices  48.3 us (31%)
  Pallas kernels  45.7 us (29%)
  starting transfers between devices  31.3 us (20%)
  blocking collectives  25.3 us (16%)
  local copies, waits for them, and re-layouts  3.32 us (2%)
  other arithmetic  2.05 us (1%)
    ppermute x3, waiting for transfers between devices, shift_lat(): return lax.ppermute(x, 'lat', [(i, (i + s) % RING) for i in range(RING)])  44.1 us
    all_to_all x1, blocking collectives, over_all(): return lax.all_to_all(x, LL, split_axis=0, concat_axis=0, tiled=True)  25.3 us
    pallas_call x2, Pallas kernels, member(): pl.pallas_call(lambda *refs: member_kernel(*refs, first=first, final=fina...  25.3 us
    all_to_all x2, starting transfers between devices, over_all(): return lax.all_to_all(x, LL, split_axis=0, concat_axis=0, tiled=True)  22.4 us
    pallas_call x1, Pallas kernels, head(): pl.pallas_call(lambda *refs: head_kernel(*refs, half=half, levels=levels,...  7.42 us
    pallas_call x1, Pallas kernels, bases(): pl.pallas_call(lambda *refs: basis_kernel(*refs, cols=cols, blocks=blocks...  7.02 us
    ppermute x3, starting transfers between devices, shift_lat(): return lax.ppermute(x, 'lat', [(i, (i + s) % RING) for i in range(RING)])  4.69 us
    ppermute x4, starting transfers between devices, swap(): return lax.ppermute(x, 'mem', SWAP)  4.21 us
  transfers between devices with their start and end apart: 9, of which 4 were waited for; matrix products, arithmetic and copies ran while one was open for 1% of the time, Pallas kernels for 17%

profile of v4, /device:TPU:1, one launch (start us, length us, event | category | flops | bytes accessed | tf_op | source)
XLA Modules:
  0.0 156.1 jit_solution(3700306898116534645)
XLA Ops:
  0.0 0.0 copy-start
  0.0 7.4 %head.1 = bf16[64,240,128]{2,1,0:T(8,128)(2,1)} custom-call(bf16[3,4,90,16,128]{4,3,2,1,0:T(8,128)(2,1)} %bitcast.17, s32[64,128]{1,0:T(8,128)} %refs_1_.1, s32[64,128]{1,0:T(8,128)} %refs_2_.1, s32[64,128]{1,0:T(8,128)} %refs_3_.1, f32[64,128]{1,0:T(8,128)} %refs_4_.1), custom_call_target="tpu_custom_call" | custom-call | flops 6000000000 | bytes 1048576 | tf_op jit(solution)/shard_map/head/pallas_call | solution.py:185
  7.4 12.2 %all-to-all-start.1 = ((bf16[64,240,128]{2,1,0:T(8,128)(2,1)}), bf16[64,240,128]{2,1,0:T(8,128)(2,1)}, u32[]{:S(2)}, u32[]{:S(2)}) async-start(bf16[64,240,128]{2,1,0:T(8,128)(2,1)} %head.1), calls=%async_computation.1 | async-start | bytes 7864320 | tf_op jit(solution)/shard_map/all_to_all | solution.py:35
  19.6 0.0 copy-done
  19.7 1.0 collective-permute-start.1
  20.7 2.6 %collective-permute-start.2 = (bf16[360,256]{1,0:T(8,128)(2,1)S(1)}, bf16[360,256]{1,0:T(8,128)(2,1)S(1)}, u32[]{:S(2)}, u32[]{:S(2)}) collective-permute-start(bf16[360,256]{1,0:T(8,128)(2,1)S(1)} %fusion), channel_id=1, source_target_pairs={{0,64},{32,96},{64,0},{96,32},{1,65},{33,97},{65,1},{97,33},{2,66}... | collective-permute-start | bytes 552968 | tf_op jit(solution)/shard_map/ppermute | solution.py:39
  23.3 1.1 collective-permute-start.3
  24.4 0.6 pad_add_fusion.refs_0_
  25.0 3.0 %relayout_last.1 = bf16[64,96,128]{2,1,0:T(8,128)(2,1)} custom-call(s32[4]{0:T(128)} %pad_add_fusion.refs_0_, bf16[3,4,90,16,128]{4,3,2,1,0:T(8,128)(2,1)} %bitcast.18), custom_call_target="tpu_custom_call" | custom-call | tf_op jit(solution)/shard_map/relayout_last/pallas_call | solution.py:225
  28.0 39.8 %collective-permute-done.1 = bf16[360,256]{1,0:T(8,128)(2,1)S(1)} collective-permute-done((bf16[360,256]{1,0:T(8,128)(2,1)S(1)}, bf16[360,256]{1,0:T(8,128)(2,1)S(1)}, u32[]{:S(2)}, u32[]{:S(2)}) %collective-permute-start.1) | collective-permute-done | bytes 184352 | tf_op jit(solution)/shard_map/ppermute | solution.py:39
  67.8 4.3 %collective-permute-done.2 = bf16[360,256]{1,0:T(8,128)(2,1)S(1)} collective-permute-done((bf16[360,256]{1,0:T(8,128)(2,1)S(1)}, bf16[360,256]{1,0:T(8,128)(2,1)S(1)}, u32[]{:S(2)}, u32[]{:S(2)}) %collective-permute-start.2) | collective-permute-done | bytes 184352 | tf_op jit(solution)/shard_map/ppermute | solution.py:39
  72.1 0.0 collective-permute-done.3
  72.1 0.1 pad_maximum_fusion.refs_1_
  72.2 1.8 %collective-permute-start.4 = (bf16[4,360,256]{2,1,0:T(8,128)(2,1)S(1)}, bf16[4,360,256]{2,1,0:T(8,128)(2,1)S(1)}, u32[]{:S(2)}, u32[]{:S(2)}) collective-permute-start(bf16[4,360,256]{2,1,0:T(8,128)(2,1)S(1)} %pad_maximum_fusion.refs_1_), channel_id=1, source_target_pairs={{0,1},{1,0},{2,3},{3,2},{4,5},{5,4},{6,7},{7,6},{8,9},{9,8},{10,11... | collective-permute-start | bytes 2211848 | tf_op jit(solution)/shard_map/ppermute | solution.py:43
  74.0 0.0 all-to-all-done.1
  74.0 10.2 %all-to-all-start = ((bf16[64,96,128]{2,1,0:T(8,128)(2,1)}), bf16[64,96,128]{2,1,0:T(8,128)(2,1)}, u32[]{:S(2)}, u32[]{:S(2)}) async-start(bf16[64,96,128]{2,1,0:T(8,128)(2,1)} %relayout_last.1), calls=%async_computation | async-start | bytes 3145728 | tf_op jit(solution)/shard_map/all_to_all | solution.py:35
  84.2 1.2 slice.4
  85.4 0.0 copy-start.4
  85.4 0.0 copy-start.1
  85.4 0.6 collective-permute-start
  86.0 7.0 %bases.1 = (bf16[768,1536]{1,0:T(8,128)(2,1)}, bf16[1536,768]{1,0:T(8,128)(2,1)}, bf16[512,512]{1,0:T(8,128)(2,1)}, bf16[512,512]{1,0:T(8,128)(2,1)}) custom-call(), custom_call_target="tpu_custom_call" | custom-call | flops 12000000000 | bytes 1048576 | tf_op jit(solution)/shard_map/bases/pallas_call | solution.py:306
  93.0 0.0 copy-done.4
  93.0 0.0 collective-permute-done.4.refs_2_
  93.0 0.0 copy-done.1
  93.0 0.8 arrange.1.refs_4_
  93.8 0.0 copy-start.3
  93.8 1.1 copy-done.3
  94.9 0.0 collective-permute-done
  94.9 0.0 copy-start.5
  94.9 0.9 copy-done.5
  95.9 15.6 %member_pair.1.refs_9_ = bf16[4,16,96,128]{3,2,1,0:T(8,128)(2,1)} custom-call(s32[4]{0:T(128)} %pad_add_fusion.refs_0_, bf16[4,16,240,128]{3,2,1,0:T(8,128)(2,1)} %bitcast.13.refs_1_, bf16[4,16,48,128]{3,2,1,0:T(8,128)(2,1)} %bitcast.20, bf16[4,16,48,128]{3,2,1,0:T(8,128)(2,1)} %bitcast.25, bf16[4,1472,128]{2,1,0:T(8,128)(2,1)} %copy-done.3, ...), custom_call_target="tpu_custom_call" | custom-call | flops 12000000000 | bytes 1048576 | tf_op jit(solution)/shard_map/member_pair/pallas_call | solution.py:546
  111.5 0.0 all-to-all-done
  111.5 9.7 %member_last.1 = (bf16[4,16,48,128]{3,2,1,0:T(8,128)(2,1)}, bf16[4,16,48,128]{3,2,1,0:T(8,128)(2,1)}) custom-call(s32[4]{0:T(128)} %pad_add_fusion.refs_0_, bf16[4,16,96,128]{3,2,1,0:T(8,128)(2,1)} %bitcast.5.refs_1_, bf16[4,16,48,128]{3,2,1,0:T(8,128)(2,1)} %bitcast.21, bf16[4,16,48,128]{3,2,1,0:T(8,128)(2,1)} %bitcast.26, bf16[4,1472,128]{2,1,0:T(8,128)(2,1)} %copy-done.3, ...), custom_call_target="tpu_custom_call" | custom-call | flops 6000000000 | bytes 1048576 | tf_op jit(solution)/shard_map/member_last/pallas_call | solution.py:546
  121.2 0.3 collective-permute-start.5
  121.5 2.3 %collective-permute-done.5 = bf16[4,16,48,128]{3,2,1,0:T(8,128)(2,1)S(1)} collective-permute-done((bf16[4,16,48,128]{3,2,1,0:T(8,128)(2,1)}, bf16[4,16,48,128]{3,2,1,0:T(8,128)(2,1)S(1)}, u32[]{:S(2)}, u32[]{:S(2)}) %collective-permute-start.5) | collective-permute-done | bytes 786464 | tf_op jit(solution)/shard_map/ppermute | solution.py:43
  123.8 0.0 copy-start.2
  123.8 1.3 add_convert_fusion
  125.2 25.3 %all_to_all.15.refs_1_ = bf16[64,48,128]{2,1,0:T(8,128)(2,1)S(1)} all-to-all(bf16[64,48,128]{2,1,0:T(8,128)(2,1)S(1)} %bitcast.19), channel_id=1, replica_groups=mesh['lat'=4,'lon'=16,'mem'=2] {'lat','lon'}, dimensions={0} | all-to-all | bytes 1572864 | tf_op jit(solution)/shard_map/all_to_all | solution.py:35
  150.5 1.6 %collective-permute-start.6 = (bf16[64,48,128]{2,1,0:T(8,128)(2,1)S(1)}, bf16[64,48,128]{2,1,0:T(8,128)(2,1)S(1)}, u32[]{:S(2)}, u32[]{:S(2)}) collective-permute-start(bf16[64,48,128]{2,1,0:T(8,128)(2,1)S(1)} %all_to_all.15.refs_1_), channel_id=1, source_target_pairs={{0,1},{1,0},{2,3},{3,2},{4,5},{5,4},{6,7},{7,6},{8,9},{9,8},{10,11... | collective-permute-start | bytes 2359304 | tf_op jit(solution)/shard_map/ppermute | solution.py:43
  152.1 1.9 %collective-permute-done.6.refs_2_ = bf16[64,48,128]{2,1,0:T(8,128)(2,1)S(1)} collective-permute-done((bf16[64,48,128]{2,1,0:T(8,128)(2,1)S(1)}, bf16[64,48,128]{2,1,0:T(8,128)(2,1)S(1)}, u32[]{:S(2)}, u32[]{:S(2)}) %collective-permute-start.6) | collective-permute-done | bytes 786464 | tf_op jit(solution)/shard_map/ppermute | solution.py:43
  154.0 0.0 copy-done.2
  154.0 2.1 %finish.1 = f32[90,16,128]{2,1,0:T(8,128)} custom-call(s32[4]{0:T(128)S(1)} %copy-done.2, bf16[64,48,128]{2,1,0:T(8,128)(2,1)S(1)} %all_to_all.15.refs_1_, bf16[64,48,128]{2,1,0:T(8,128)(2,1)S(1)} %collective-permute-done.6.refs_2_), custom_call_target="tpu_custom_call" | custom-call | tf_op jit(solution)/shard_map/finish/pallas_call | solution.py:581
  (2 shorter events, 0.1 us)
Async XLA Ops:
  0.0 19.6 %copy-start = (f32[1,360,512]{2,1,0:T(8,128)S(1)}, f32[1,360,512]{2,1,0:T(8,128)}, u32[]{:S(2)}) copy-start(f32[1,360,512]{2,1,0:T(8,128)} %param.7) | copy-start | bytes 2211844
  7.4 66.6 %all-to-all-start.1 = ((bf16[64,240,128]{2,1,0:T(8,128)(2,1)}), bf16[64,240,128]{2,1,0:T(8,128)(2,1)}, u32[]{:S(2)}, u32[]{:S(2)}) async-start(bf16[64,240,128]{2,1,0:T(8,128)(2,1)} %head.1), calls=%async_computation.1 | async-start | bytes 7864320 | tf_op jit(solution)/shard_map/all_to_all | solution.py:35
  19.7 48.1 %collective-permute-start.1 = (bf16[360,256]{1,0:T(8,128)(2,1)S(1)}, bf16[360,256]{1,0:T(8,128)(2,1)S(1)}, u32[]{:S(2)}, u32[]{:S(2)}) collective-permute-start(bf16[360,256]{1,0:T(8,128)(2,1)S(1)} %fusion), channel_id=1, source_target_pairs={{0,32},{32,64},{64,96},{96,0},{1,33},{33,65},{65,97},{97,1},{2,34}... | collective-permute-start | bytes 552968 | tf_op jit(solution)/shard_map/ppermute | solution.py:39
  20.7 51.4 %collective-permute-start.2 = (bf16[360,256]{1,0:T(8,128)(2,1)S(1)}, bf16[360,256]{1,0:T(8,128)(2,1)S(1)}, u32[]{:S(2)}, u32[]{:S(2)}) collective-permute-start(bf16[360,256]{1,0:T(8,128)(2,1)S(1)} %fusion), channel_id=1, source_target_pairs={{0,64},{32,96},{64,0},{96,32},{1,65},{33,97},{65,1},{97,33},{2,66}... | collective-permute-start | bytes 552968 | tf_op jit(solution)/shard_map/ppermute | solution.py:39
  23.3 48.8 %collective-permute-start.3 = (bf16[360,256]{1,0:T(8,128)(2,1)S(1)}, bf16[360,256]{1,0:T(8,128)(2,1)S(1)}, u32[]{:S(2)}, u32[]{:S(2)}) collective-permute-start(bf16[360,256]{1,0:T(8,128)(2,1)S(1)} %fusion), channel_id=1, source_target_pairs={{0,96},{32,0},{64,32},{96,64},{1,97},{33,1},{65,33},{97,65},{2,98}... | collective-permute-start | bytes 552968 | tf_op jit(solution)/shard_map/ppermute | solution.py:39
  72.2 20.8 %collective-permute-start.4 = (bf16[4,360,256]{2,1,0:T(8,128)(2,1)S(1)}, bf16[4,360,256]{2,1,0:T(8,128)(2,1)S(1)}, u32[]{:S(2)}, u32[]{:S(2)}) collective-permute-start(bf16[4,360,256]{2,1,0:T(8,128)(2,1)S(1)} %pad_maximum_fusion.refs_1_), channel_id=1, source_target_pairs={{0,1},{1,0},{2,3},{3,2},{4,5},{5,4},{6,7},{7,6},{8,9},{9,8},{10,11... | collective-permute-start | bytes 2211848 | tf_op jit(solution)/shard_map/ppermute | solution.py:43
  74.0 37.5 %all-to-all-start = ((bf16[64,96,128]{2,1,0:T(8,128)(2,1)}), bf16[64,96,128]{2,1,0:T(8,128)(2,1)}, u32[]{:S(2)}, u32[]{:S(2)}) async-start(bf16[64,96,128]{2,1,0:T(8,128)(2,1)} %relayout_last.1), calls=%async_computation | async-start | bytes 3145728 | tf_op jit(solution)/shard_map/all_to_all | solution.py:35
  85.4 7.6 %copy-start.4 = (bf16[64,48,128]{2,1,0:T(8,128)(2,1)}, bf16[64,48,128]{2,1,0:T(8,128)(2,1)S(1)}, u32[]{:S(2)}) copy-start(bf16[64,48,128]{2,1,0:T(8,128)(2,1)S(1)} %slice.4) | copy-start | bytes 2359300
  85.4 7.6 %copy-start.1 = (s32[4]{0:T(128)S(1)}, s32[4]{0:T(128)}, u32[]{:S(2)}) copy-start(s32[4]{0:T(128)} %pad_add_fusion.refs_0_) | copy-start | bytes 52
  85.4 9.6 %collective-permute-start = (bf16[64,48,128]{2,1,0:T(8,128)(2,1)S(1)}, bf16[64,48,128]{2,1,0:T(8,128)(2,1)S(1)}, u32[]{:S(2)}, u32[]{:S(2)}) collective-permute-start(bf16[64,48,128]{2,1,0:T(8,128)(2,1)S(1)} %slice.4), channel_id=1, source_target_pairs={{0,1},{1,0},{2,3},{3,2},{4,5},{5,4},{6,7},{7,6},{8,9},{9,8},{10,11... | collective-permute-start | bytes 2359304 | tf_op jit(solution)/shard_map/ppermute | solution.py:43
  93.8 1.1 copy-start.3
  94.9 0.9 copy-start.5
  121.2 2.6 %collective-permute-start.5 = (bf16[4,16,48,128]{3,2,1,0:T(8,128)(2,1)}, bf16[4,16,48,128]{3,2,1,0:T(8,128)(2,1)S(1)}, u32[]{:S(2)}, u32[]{:S(2)}) collective-permute-start(bf16[4,16,48,128]{3,2,1,0:T(8,128)(2,1)} %get-tuple-element.20), channel_id=1, source_target_pairs={{0,1},{1,0},{2,3},{3,2},{4,5},{5,4},{6,7},{7,6},{8,9},{9,8},{10,11... | collective-permute-start | bytes 2359304 | tf_op jit(solution)/shard_map/ppermute | solution.py:43
  123.8 30.2 %copy-start.2 = (s32[4]{0:T(128)S(1)}, s32[4]{0:T(128)}, u32[]{:S(2)}) copy-start(s32[4]{0:T(128)} %pad_add_fusion.refs_0_) | copy-start | bytes 52
  150.5 3.5 %collective-permute-start.6 = (bf16[64,48,128]{2,1,0:T(8,128)(2,1)S(1)}, bf16[64,48,128]{2,1,0:T(8,128)(2,1)S(1)}, u32[]{:S(2)}, u32[]{:S(2)}) collective-permute-start(bf16[64,48,128]{2,1,0:T(8,128)(2,1)S(1)} %all_to_all.15.refs_1_), channel_id=1, source_target_pairs={{0,1},{1,0},{2,3},{3,2},{4,5},{5,4},{6,7},{7,6},{8,9},{9,8},{10,11... | collective-permute-start | bytes 2359304 | tf_op jit(solution)/shard_map/ppermute | solution.py:43
